TPU v7x, 512 devices: a whole 4x8x8 slice. The times are simulated.
512 devices in a mesh: tok: 32 (over z_hi, y), voc: 16 (over z_lo, x, core).
Axes of the slice: x: 4, y: 8, z: 8 (z_hi: 4, z_lo: 2; z = z_hi * 2 + z_lo), core: 2. Of those that a mesh axis runs over, the one named last changes fastest.
Arguments:
- hidden: bfloat16 [4096, 2048], P('tok'), may hold values from -6 to 6
- mix_weight: bfloat16 [4, 2048], P(None, 'voc'), may hold values from -0.0546875 to 0.0546875
- comp_proj: bfloat16 [2048, 4, 2048], P(None, None, 'voc'), may hold values from -0.110485435 to 0.110485435
- vocab_weight: bfloat16 [2048, 4096], P(None, 'voc'), may hold values from -0.625 to 0.625
- log_normalizer: float32 [4, 4096], P(None, 'tok'), may hold values from 11 to 11.6
- targets: int32 [4096], P('tok'), may hold values from 0 to 4095
- loss_grad: float32 [4096], P('tok'), may hold values from 0.5 to 1.5
Outputs:
- hidden_grad: bfloat16 [4096, 2048], P('tok', 'voc')
- proj_grad: bfloat16 [2048, 4, 2048], P('tok', None, 'voc')
- vocab_grad: bfloat16 [2048, 4096], P('tok', 'voc')
All inputs are finite; a program needn't handle non-finite values.
Results may differ from a plain program's by a relative error of at most 0.02.
Values may be sent and summed in bfloat16 or wider, within the bound.
A program may use at most 64 MiB of HBM per device.

v0:
```python
import jax
import jax.numpy as jnp
from jax import lax
from jax.sharding import Mesh
from jax.sharding import PartitionSpec as P

TOK = ("tok_0", "tok_1")


def copy_for_each(x, axis):
    count = lax.axis_size(axis)
    return lax.all_to_all(jnp.broadcast_to(x[None], (count, *x.shape)), axis, 0, 0, tiled=True)


def taken_together(x, axis):
    everything = copy_for_each(x, axis)
    return jnp.sum(everything, axis=0)


def together(arrays, axis):
    vector, at, done = (jnp.concatenate([a.reshape(-1) for a in arrays]), 0, [])
    subtotal = taken_together(vector, axis)
    for a in arrays:
        done.append(subtotal[at : at + a.size].reshape(a.shape))
        at += a.size
    return tuple(done)


def own_block(tiles, axes, order):
    dims = [lax.axis_size(a) for a in axes]
    tiles = tiles.reshape(*dims, *tiles.shape[1:])
    tiles = tiles.transpose(*order, *range(len(axes), tiles.ndim))
    tiles = tiles.reshape(-1, *tiles.shape[len(axes) :])
    for k in order:
        tiles = lax.psum_scatter(tiles, axes[k], scatter_dimension=0, tiled=True)
    return tiles[0]


def split_up(x, dim, count):
    before, after = (x.shape[:dim], x.shape[dim + 1 :])
    return jnp.moveaxis(x.reshape(*before, count, -1, *after), dim, 0)


def scatter_axes(x, axes, order, dim):
    count = lax.axis_size(axes)
    return own_block(split_up(x, dim, count), axes, order)


def sent_and_summed(x, axis, dim):
    count = lax.axis_size(axis)
    tiles = lax.all_to_all(split_up(x, dim, count), axis, 0, 0, tiled=True)
    return jnp.sum(tiles.astype(jnp.float32), axis=0)


def body(hidden, mix_weight, comp_proj, vocab_weight, log_normalizer, targets, loss_grad):
    voc_place = lax.axis_index("voc")
    tok_count = lax.axis_size(TOK)
    model_width = hidden.shape[1]
    components = comp_proj.shape[1]
    own_cols = comp_proj.shape[2]
    own_vocab = vocab_weight.shape[1]
    pre_act = jnp.einsum("td,dke->ekt", hidden, comp_proj, preferred_element_type=jnp.float32)
    context_own = jnp.tanh(pre_act).astype(jnp.bfloat16)
    own_hidden = lax.dynamic_slice_in_dim(hidden, voc_place * own_cols, own_cols, 1)
    mixing_part = jnp.einsum(
        "kd,td->kt", mix_weight, own_hidden, preferred_element_type=jnp.float32
    )
    context_full = lax.all_gather(context_own, "voc", axis=0, tiled=True)
    logits = jnp.einsum(
        "dkt,dv->ktv", context_full, vocab_weight, preferred_element_type=jnp.float32
    )
    vocab_ids = voc_place * own_vocab + lax.iota(jnp.int32, own_vocab)
    onehot = (targets[:, None] == vocab_ids[None, :]).astype(jnp.float32)
    target_part = jnp.sum(logits * onehot[None], axis=2)
    target, mixing = together((target_part, mixing_part), "voc")
    exp_mix = jnp.exp(mixing)
    weights = exp_mix / jnp.sum(exp_mix, axis=0, keepdims=True)
    likely = jnp.exp(target - log_normalizer)
    joint_mass = weights * likely
    posterior = joint_mass / jnp.sum(joint_mass, axis=0, keepdims=True)
    factor = loss_grad[None, :] * posterior
    logit_grad = (
        factor[:, :, None] * (jnp.exp(logits - log_normalizer[:, :, None]) - onehot[None])
    ).astype(jnp.bfloat16)
    mixing_grad = loss_grad[None, :] * (weights - posterior)
    rows_part = context_full
    vocab_grad = (
        scatter_axes(
            jnp.einsum(
                "dkt,ktv->dv", rows_part, logit_grad, preferred_element_type=jnp.float32
            ).astype(jnp.bfloat16),
            TOK,
            (1, 0),
            0,
        )
        .astype(jnp.float32)
        .astype(jnp.bfloat16)
    )
    rows_part = vocab_weight
    context_grad = sent_and_summed(
        jnp.einsum("dv,ktv->dkt", rows_part, logit_grad, preferred_element_type=jnp.float32).astype(
            jnp.bfloat16
        ),
        "voc",
        0,
    )
    own_f = context_own.astype(jnp.float32)
    pre_grad = (context_grad * (1.0 - own_f * own_f)).astype(jnp.bfloat16)
    rows_part = comp_proj
    hidden_sum = sent_and_summed(
        jnp.einsum("jke,ekt->jt", rows_part, pre_grad, preferred_element_type=jnp.float32).astype(
            jnp.bfloat16
        ),
        "voc",
        0,
    )
    mix_term = jnp.einsum(
        "kt,kd->td", mixing_grad, mix_weight.astype(jnp.float32), precision=lax.Precision.HIGHEST
    )
    hidden_grad = (hidden_sum.T + mix_term).astype(jnp.bfloat16)
    partial_sum = jnp.einsum("tr,ekt->rke", hidden, pre_grad, preferred_element_type=jnp.float32)
    received = lax.all_to_all(
        partial_sum.astype(jnp.bfloat16), TOK, split_axis=0, concat_axis=1, tiled=True
    ).astype(partial_sum.dtype)
    proj_sum = jnp.sum(
        received.reshape(model_width // tok_count, tok_count, components, own_cols), axis=1
    )
    proj_grad = proj_sum.astype(jnp.bfloat16)
    return (hidden_grad, proj_grad, vocab_grad)


def solution(mesh):
    split = Mesh(mesh.devices.reshape(4, 8, mesh.shape["voc"]), ("tok_0", "tok_1", "voc"))
    in_specs = (
        P(TOK, None),
        P(None, "voc"),
        P(None, None, "voc"),
        P(None, "voc"),
        P(None, TOK),
        P(TOK),
        P(TOK),
    )
    out_specs = (P(TOK, "voc"), P(TOK, None, "voc"), P(TOK, "voc"))
    return jax.shard_map(body, mesh=split, in_specs=in_specs, out_specs=out_specs, check_vma=False)
```

profile of v0, /device:TPU:1, one launch (start us, length us, event | category | flops | bytes accessed | tf_op | source)
XLA Modules:
  0.0 237.1 jit_solution(2281469979750393927)
XLA Ops:
  7.2 0.0 copy-start
  7.2 0.0 copy-start.9
  7.2 0.0 copy-start.13
  7.2 0.0 all-gather.2.cloned.1.call-start
  7.2 3.2 %fusion.16 = bf16[128,4,128]{2,0,1:T(8,128)(2,1)} fusion(bf16[2048,4,128]{2,1,0:T(4,128)(2,1)} %param.9, bf16[128,2048]{1,0:T(8,128)(2,1)} %param.7), kind=kOutput, calls=%fused_computation.16 | convolution fusion | flops 268500992 | bytes 2752512 | tf_op jit(solution)/shard_map/td,dke->ekt/dot_general | solution.py:62
  10.4 0.0 all-gather.2.cloned.1.call-update
  10.5 0.0 copy-done.9
  10.5 0.9 convolution_bitcast_fusion.2
  11.4 0.0 copy-done.13
  11.4 0.0 copy-start.4
  11.4 0.0 copy-start.11
  11.4 0.1 compare_convert_fusion
  11.5 44.2 %all-gather.2.cloned.1.call-done = bf16[2048,4,128]{2,0,1:T(8,128)(2,1)} async-done(((bf16[128,4,128]{2,0,1:T(8,128)(2,1)}), bf16[2048,4,128]{2,0,1:T(8,128)(2,1)}) %all-gather.2.cloned.1.call-update) | async-done | bytes 2097168 | tf_op jit(solution)/shard_map/all_gather | solution.py:68
  55.6 0.0 copy-done
  55.6 2.4 %multiply_reduce_fusion = (f32[4,128]{1,0:T(4,128)S(1)}, f32[4,128,256]{2,1,0:T(8,128)S(1)}) fusion(f32[128,256]{1,0:T(8,128)S(1)} %compare_convert_fusion, bf16[2048,4,128]{2,0,1:T(8,128)(2,1)} %all-gather.2.cloned.1.call-done, bf16[2048,256]{1,0:T(8,128)(2,1)S(1)} %copy-done), kind=kOutput, calls=%fused_computation.28 | convolution fusion | flops 537132544 | bytes 3803136 | tf_op jit(solution)/shard_map/dkt,dv->ktv/dot_general | solution.py:69
  58.1 0.0 copy-start.2
  58.1 10.1 %all_to_all.28 = f32[16,1,1024]{2,1,0:T(1,128)S(1)} all-to-all(f32[16,1,1024]{2,1,0:T(1,128)S(1)} %broadcast_in_dim.2), channel_id=1, replica_groups=mesh['tok_0'=4,'tok_1'=8,'voc'=16] {'voc'}, dimensions={0} | all-to-all | bytes 131072 | tf_op jit(solution)/shard_map/all_to_all | solution.py:12
  68.2 0.1 reduce_sum.67
  68.3 0.0 copy-done.4
  68.3 0.0 copy-start.5
  68.3 0.0 copy-start.7
  68.3 0.5 copy-done.5
  68.8 0.0 copy-done.11
  68.8 0.8 fusion.6
  69.6 0.6 copy.81
  70.2 0.0 copy-done.2
  70.2 0.0 copy-done.7
  70.2 29.5 %all_to_all.29 = bf16[16,128,4,128]{1,3,2,0:T(8,128)(2,1)S(1)} all-to-all(bf16[16,128,4,128]{1,3,2,0:T(8,128)(2,1)S(1)} %bitcast.73), channel_id=1, replica_groups=mesh['tok_0'=4,'tok_1'=8,'voc'=16] {'voc'}, dimensions={0} | all-to-all | bytes 4194304 | tf_op jit(solution)/shard_map/all_to_all | solution.py:51
  99.7 0.0 copy-start.3
  99.7 1.1 convert_reduce_fusion
  100.8 1.1 copy.50
  101.9 0.0 copy-done.3
  101.9 1.7 fusion.7
  103.6 0.9 copy.82
  104.6 5.2 %all-to-all-start.2 = ((bf16[16,128,128]{1,2,0:T(8,128)(2,1)}), bf16[16,128,128]{1,2,0:T(8,128)(2,1)}, u32[]{:S(2)}, u32[]{:S(2)}) async-start(bf16[16,128,128]{1,2,0:T(8,128)(2,1)} %bitcast.72), calls=%async_computation.2 | async-start | bytes 1048576 | tf_op jit(solution)/shard_map/all_to_all | solution.py:51
  109.8 1.8 fusion
  111.6 2.5 %copy.54 = bf16[2048,4,128]{2,1,0:T(4,128)(2,1)} copy(bf16[2048,4,128]{0,2,1:T(8,128)(2,1)S(1)} %fusion) | data formatting | bytes 4194304 | tf_op jit(solution)/shard_map/convert_element_type | solution.py:123
  114.2 0.0 copy-start.1
  114.2 5.5 %all-to-all-done.2 = bf16[16,128,128]{1,2,0:T(8,128)(2,1)} async-done(((bf16[16,128,128]{1,2,0:T(8,128)(2,1)}), bf16[16,128,128]{1,2,0:T(8,128)(2,1)}, u32[]{:S(2)}, u32[]{:S(2)}) %all-to-all-start.2) | async-done | bytes 524320 | tf_op jit(solution)/shard_map/all_to_all | solution.py:51
  119.7 11.5 %all-to-all-start.3 = ((bf16[2048,4,128]{2,1,0:T(4,128)(2,1)}), bf16[2048,4,128]{2,1,0:T(4,128)(2,1)}, u32[]{:S(2)}, u32[]{:S(2)}) async-start(bf16[2048,4,128]{2,1,0:T(4,128)(2,1)} %copy.54), calls=%async_computation.3 | async-start | bytes 4194304 | tf_op jit(solution)/shard_map/all_to_all | solution.py:122
  131.2 0.0 reduce-scatter.3.cloned.1.call-start
  131.2 0.0 copy-done.1
  131.2 1.9 fusion.1
  133.1 0.0 copy-start.6
  133.2 0.0 copy-start.8
  133.2 0.0 copy-start.10
  133.2 0.0 copy-start.12
  133.2 1.1 copy.56
  134.3 0.0 reduce-scatter.3.cloned.1.call-update
  134.3 0.0 reduce-scatter.5.cloned.1.call-start
  134.3 57.7 %reduce-scatter.3.cloned.1.call-done = bf16[4,64,256]{2,1,0:T(8,128)(2,1)} async-done(((bf16[32,64,256]{2,1,0:T(8,128)(2,1)}), bf16[4,64,256]{2,1,0:T(8,128)(2,1)}) %reduce-scatter.3.cloned.1.call-update) | async-done | bytes 131088 | tf_op jit(solution)/shard_map/reduce_scatter | solution.py:35
  192.0 0.0 reduce-scatter.5.cloned.1.call-update
  192.1 1.1 convert_reduce_fusion.1
  193.2 0.0 copy-done.6
  193.2 0.0 copy-done.8
  193.2 0.0 copy-done.10
  193.2 0.0 copy-done.12
  193.2 0.9 fusion.19
  194.1 4.2 %all-to-all-done.3 = bf16[2048,4,128]{2,1,0:T(4,128)(2,1)} async-done(((bf16[2048,4,128]{2,1,0:T(4,128)(2,1)}), bf16[2048,4,128]{2,1,0:T(4,128)(2,1)}, u32[]{:S(2)}, u32[]{:S(2)}) %all-to-all-start.3) | async-done | bytes 2097184 | tf_op jit(solution)/shard_map/all_to_all | solution.py:122
  198.3 3.1 %reduce.3 = bf16[64,4,128]{2,1,0:T(4,128)(2,1)} reduce(bf16[32,64,4,128]{3,2,1,0:T(4,128)(2,1)} %bitcast.14, bf16[]{:T(256)} %constant.17.clone.1), dimensions={0}, to_apply=%region_6.0 | reduce | flops 1015808 | bytes 2162690
  201.4 29.2 %reduce-scatter.5.cloned.1.call-done = bf16[1,64,256]{2,1,0:T(8,128)(2,1)} async-done(((bf16[4,64,256]{2,1,0:T(8,128)(2,1)}), bf16[1,64,256]{2,1,0:T(8,128)(2,1)}) %reduce-scatter.5.cloned.1.call-update) | async-done | bytes 32784 | tf_op jit(solution)/shard_map/reduce_scatter | solution.py:35
  (6 shorter events, 0.1 us)
Async XLA Ops:
  7.2 48.5 %copy-start = (bf16[2048,256]{1,0:T(8,128)(2,1)S(1)}, bf16[2048,256]{1,0:T(8,128)(2,1)}, u32[]{:S(2)}) copy-start(bf16[2048,256]{1,0:T(8,128)(2,1)} %param.10) | copy-start | bytes 3145732
  7.2 3.3 %copy-start.9 = (bf16[4,128]{1,0:T(4,128)(2,1)S(1)}, bf16[4,128]{1,0:T(4,128)(2,1)}, u32[]{:S(2)}) copy-start(bf16[4,128]{1,0:T(4,128)(2,1)} %param.8) | copy-start | bytes 3076
  7.2 4.2 %copy-start.13 = (s32[128]{0:T(128)S(1)}, s32[128]{0:T(128)}, u32[]{:S(2)}) copy-start(s32[128]{0:T(128)} %param.12) | copy-start | bytes 1540
  7.2 48.4 %all-gather.2.cloned.1.call-start = ((), (), s32[]{:S(2)}) async-start(), calls=%async_computation.6 | async-start | bytes 2228224 | tf_op jit(solution)/shard_map/all_gather | solution.py:68
  11.4 56.9 %copy-start.4 = (f32[4,128]{1,0:T(4,128)S(1)}, f32[4,128]{1,0:T(4,128)}, u32[]{:S(2)}) copy-start(f32[4,128]{1,0:T(4,128)} %param.11) | copy-start | bytes 6148
  11.4 57.4 %copy-start.11 = (f32[128]{0:T(128)S(1)}, f32[128]{0:T(128)}, u32[]{:S(2)}) copy-start(f32[128]{0:T(128)} %param.13) | copy-start | bytes 1540
  58.1 12.1 %copy-start.2 = (f32[4,128,256]{2,1,0:T(8,128)}, f32[4,128,256]{2,1,0:T(8,128)S(1)}, u32[]{:S(2)}) copy-start(f32[4,128,256]{2,1,0:T(8,128)S(1)} %get-tuple-element.15) | copy-start | bytes 1572868
  68.3 0.5 copy-start.5
  68.3 1.9 copy-start.7
  99.7 2.2 copy-start.3
  104.6 15.1 %all-to-all-start.2 = ((bf16[16,128,128]{1,2,0:T(8,128)(2,1)}), bf16[16,128,128]{1,2,0:T(8,128)(2,1)}, u32[]{:S(2)}, u32[]{:S(2)}) async-start(bf16[16,128,128]{1,2,0:T(8,128)(2,1)} %bitcast.72), calls=%async_computation.2 | async-start | bytes 1048576 | tf_op jit(solution)/shard_map/all_to_all | solution.py:51
  114.2 17.0 %copy-start.1 = (bf16[2048,4,128]{2,0,1:T(8,128)(2,1)S(1)}, bf16[2048,4,128]{2,0,1:T(8,128)(2,1)}, u32[]{:S(2)}) copy-start(bf16[2048,4,128]{2,0,1:T(8,128)(2,1)} %all-gather.2.cloned.1.call-done) | copy-start | bytes 6291460
  119.7 78.6 %all-to-all-start.3 = ((bf16[2048,4,128]{2,1,0:T(4,128)(2,1)}), bf16[2048,4,128]{2,1,0:T(4,128)(2,1)}, u32[]{:S(2)}, u32[]{:S(2)}) async-start(bf16[2048,4,128]{2,1,0:T(4,128)(2,1)} %copy.54), calls=%async_computation.3 | async-start | bytes 4194304 | tf_op jit(solution)/shard_map/all_to_all | solution.py:122
  131.2 60.9 %reduce-scatter.3.cloned.1.call-start = ((), (), s32[]{:S(2)}) async-start(), calls=%async_computation.7 | async-start | bytes 1179648 | tf_op jit(solution)/shard_map/reduce_scatter | solution.py:35
  133.1 60.0 %copy-start.6 = (f32[128]{0:T(128)S(1)}, f32[128]{0:T(128)}, u32[]{:S(2)}) copy-start(f32[128]{0:T(128)} %copy-done.5) | copy-start | bytes 1540
  133.2 60.0 %copy-start.8 = (f32[128]{0:T(128)S(1)}, f32[128]{0:T(128)}, u32[]{:S(2)}) copy-start(f32[128]{0:T(128)} %copy-done.7) | copy-start | bytes 1540
  133.2 60.0 %copy-start.10 = (bf16[4,128]{1,0:T(4,128)(2,1)S(1)}, bf16[4,128]{1,0:T(4,128)(2,1)}, u32[]{:S(2)}) copy-start(bf16[4,128]{1,0:T(4,128)(2,1)} %param.8) | copy-start | bytes 3076
  133.2 60.0 %copy-start.12 = (f32[128]{0:T(128)S(1)}, f32[128]{0:T(128)}, u32[]{:S(2)}) copy-start(f32[128]{0:T(128)} %param.13) | copy-start | bytes 1540
  134.3 96.3 %reduce-scatter.5.cloned.1.call-start = ((), (), s32[]{:S(2)}) async-start(), calls=%async_computation.8 | async-start | bytes 163840 | tf_op jit(solution)/shard_map/reduce_scatter | solution.py:35
Sparse Core Ops, SparseCore 0:
  10.6 45.0 all-gather.1
  134.8 57.1 reduce-scatter.2
  195.4 35.1 reduce-scatter.4
where the time goes:
time: 239 us; the launch traced here: 237 us
  waiting for transfers between devices  141 us (59%)
  blocking collectives  39.6 us (17%)
  starting transfers between devices  16.8 us (7%)
  between operations  14 us (6%)
  matrix products  13.6 us (6%)
  local copies, waits for them, and re-layouts  6.79 us (3%)
  other arithmetic  5.54 us (2%)
    reduce_scatter x2, waiting for transfers between devices, own_block(): tiles = lax.psum_scatter(tiles, axes[k], scatter_dimension=0, tiled=True)  86.9 us
    all_gather x1, waiting for transfers between devices, body(): context_full = lax.all_gather(context_own, 'voc', axis=0, tiled=True)  44.2 us
    all_to_all x1, blocking collectives, sent_and_summed(): tiles = lax.all_to_all(split_up(x, dim, count), axis, 0, 0, tiled=True)  29.5 us
    all_to_all x1, starting transfers between devices, body(): lax.all_to_all(partial_sum.astype(jnp.bfloat16), TOK, split_axis=0, conca...  11.5 us
    all_to_all x1, blocking collectives, copy_for_each(): lax.all_to_all(jnp.broadcast_to(x[None], (count, *x.shape)), axis, 0, 0,...  10.1 us
    all_to_all x1, waiting for transfers between devices, sent_and_summed(): tiles = lax.all_to_all(split_up(x, dim, count), axis, 0, 0, tiled=True)  5.49 us
    all_to_all x1, starting transfers between devices, sent_and_summed(): tiles = lax.all_to_all(split_up(x, dim, count), axis, 0, 0, tiled=True)  5.23 us
  transfers between devices with their start and end apart: 5, of which 5 were waited for; matrix products, arithmetic and copies ran while one was open for 6% of the time, Pallas kernels for 0%

commit v1 on v0

v1 whole, which is shorter than its diff:
```python
import jax
import jax.numpy as jnp
from jax import lax
from jax.experimental import pallas as pl
from jax.experimental.pallas import tpu as pltpu
from jax.sharding import Mesh
from jax.sharding import PartitionSpec as P

MESH = pl.DeviceIdType.MESH
BF, F32 = jnp.bfloat16, jnp.float32
ZH, Y, ZL, X, C = 4, 8, 2, 4, 2
D, K, T, V, E = 2048, 4, 128, 256, 128
N_SEND, N_RECV = 260, 230
ORDER = (0, 2, 1, 3)

NT = (((1,), (1,)), ((), ()))
TN = (((0,), (0,)), ((), ()))


def mm(a, b):
    return jnp.dot(a, b, preferred_element_type=F32)


def mm_nt(a, b):
    return lax.dot_general(a, b, NT, preferred_element_type=F32)


class Net:
    def __init__(self, send_sems, recv_sems):
        self.send_sems, self.recv_sems = send_sems, recv_sems
        self.roles, self.sent = {}, []

    def slot(self, role):
        return self.recv_sems.at[self.roles.setdefault(role, len(self.roles))]

    def send(self, src, dst, role, device):
        copy = pltpu.make_async_remote_copy(
            src_ref=src,
            dst_ref=dst,
            send_sem=self.send_sems.at[len(self.sent)],
            recv_sem=self.slot(role),
            device_id=device,
            device_id_type=MESH,
        )
        copy.start()
        self.sent.append(copy)

    def got(self, dst, role):
        pltpu.make_async_remote_copy(
            src_ref=dst,
            dst_ref=dst,
            send_sem=self.send_sems.at[0],
            recv_sem=self.slot(role),
            device_id={"c": 1 - lax.axis_index("c")},
            device_id_type=MESH,
        ).wait_recv()

    def finish(self):
        for copy in self.sent:
            copy.wait_send()


def kernel(
    hid_hbm, cp_hbm, w_hbm, mw_ref, ln_ref, tg_ref, loss_ref,
    hg_ref, pg_ref, vg_ref,
    hid, cpraw, stage, cp, w, wt, wp, ctx, eb, lgt, lgp, arx,
    cgb, r2, sp, rxm, rxp, xs, zs, zr, pgz, pgs, hx, ht, pp, prx, pst,
    hpb, hrx, vgb, vrx, vzs, vzr,
    send_sems, recv_sems, local_sems,
):
    zh, y = lax.axis_index("zh"), lax.axis_index("y")
    zl, x, c = lax.axis_index("zl"), lax.axis_index("x"), lax.axis_index("c")
    voc = zl * 8 + x * 2 + c
    net = Net(send_sems, recv_sems)

    def xat(dx):
        return lax.rem(x + dx + X, X)

    def yat(dy):
        return lax.rem(y + dy, Y)

    def zat(dz):
        return lax.rem(zh + dz, ZH)

    def peer(dl, dx, dc):
        return {"zl": (zl + dl) % 2, "x": xat(dx), "c": (c + dc) % 2}

    def lanes(k):
        return pl.ds(k * T, T)

    right, left = {"x": xat(1)}, {"x": xat(-1)}
    other, over = {"c": 1 - c}, {"zl": 1 - zl}
    voc_peers = [(dl, dx, dc) for dl in range(2) for dx in range(4) for dc in range(2)][1:]

    parts = 4
    rows = D * K // parts
    loads = [pltpu.make_async_copy(hid_hbm, hid, local_sems.at[0])]
    for q in range(parts):
        span = pl.ds(q * rows, rows)
        loads.append(pltpu.make_async_copy(cp_hbm.at[span], cpraw.at[span], local_sems.at[1 + q]))
    loads.append(pltpu.make_async_copy(w_hbm, w, local_sems.at[1 + parts]))
    for load in loads:
        load.start()
    barrier = pltpu.get_barrier_semaphore()
    greeted = [peer(*p) for p in voc_peers]
    greeted += [{"y": yat(dy)} for dy in range(1, Y)] + [{"zh": zat(dz)} for dz in range(1, ZH)]
    for device in greeted:
        pl.semaphore_signal(barrier, inc=1, device_id=device, device_id_type=MESH)

    loads[0].wait()
    pre = jnp.zeros((T, K * E), F32)
    for q in range(parts):
        loads[1 + q].wait()
        stage[...] = cpraw[pl.ds(q * rows, rows), :].astype(F32)
        span = pl.ds(q * (D // parts), D // parts)
        for k in range(K):
            cp[span, lanes(k)] = stage[pl.ds(k, D // parts, stride=K), :].astype(BF)
        pre = pre + mm(hid[:, span], cp[span, :])
    acts = jnp.tanh(pre)

    def block(dl, dx, dc, k):
        at = (zl + dl) % 2 * 8 + xat(dx) * 2 + (c + dc) % 2
        return ctx.at[pl.ds(pl.multiple_of(at * E, E), E), lanes(k)]

    for k in range(K):
        ctx[pl.ds(pl.multiple_of(voc * E, E), E), lanes(k)] = acts[:, k * E : (k + 1) * E].T.astype(BF)
    mw = jnp.concatenate([mw_ref[...].astype(F32), jnp.zeros((4, E), F32)], axis=0)
    own_hid = hid[:, pl.ds(pl.multiple_of(voc * E, E), E)]
    mix_part = mm_nt(mw.astype(BF), own_hid)

    pl.semaphore_wait(barrier, len(greeted))

    def push(dl, dx, k, role, device):
        net.send(block(dl, dx, 0, k), block(dl, dx, 0, k), role, device)

    for k in range(K):
        push(0, 0, k, ("ag", 1, 0, k), over)
        push(0, 0, k, ("ag", 0, -1, k), right)
        push(0, 0, k, ("ag", 0, 1, k), left)
        push(0, 0, k, ("ac", 0, 0, k), other)
    loads[1 + parts].wait()
    net.send(w.at[:, 1 - c], wp, ("wp",), other)
    for j in range(16):
        wt[:, j * 128 : (j + 1) * 128] = w[j // 2, j % 2].T

    def from_left(dl, k):
        net.got(block(dl, -1, 0, k), ("ag", dl, -1, k))
        if k < 2:
            push(dl, -1, k, ("ag", dl, 2, k), right)
        push(dl, -1, k, ("ac", dl, -1, k), other)

    def from_right(dl, k):
        net.got(block(dl, 1, 0, k), ("ag", dl, 1, k))
        if k >= 2:
            push(dl, 1, k, ("ag", dl, 2, k), left)
        push(dl, 1, k, ("ac", dl, 1, k), other)

    def from_far(dl, k):
        net.got(block(dl, 2, 0, k), ("ag", dl, 2, k))
        push(dl, 2, k, ("ac", dl, 2, k), other)

    for k in range(K):
        net.got(block(1, 0, 0, k), ("ag", 1, 0, k))
        push(1, 0, k, ("ag", 1, -1, k), right)
        push(1, 0, k, ("ag", 1, 1, k), left)
        push(1, 0, k, ("ac", 1, 0, k), other)
        from_left(0, k)
        from_right(0, k)
    for dz in (1, 3, 2):
        span = pl.ds(pl.multiple_of(zat(dz) * 512, 512), 512)
        net.send(hid.at[:, span], hx.at[dz], ("hx", dz), {"zh": zat(dz)})
    hx[0] = hid[:, pl.ds(pl.multiple_of(zh * 512, 512), 512)]
    for k in range(K):
        from_left(1, k)
        from_right(1, k)
        from_far(0, k)

    ids = lax.broadcasted_iota(jnp.int32, (V, T), 0) + voc * V
    hit = ids == tg_ref[...]
    targets = []
    for k in range(K):
        from_far(1, k)
        for dl in range(2):
            for dx in (0, -1, 1, 2):
                net.got(block(dl, dx, 1, k), ("ac", dl, dx, k))
        logits = mm(wt[...], ctx[:, lanes(k)])
        targets.append(jnp.sum(jnp.where(hit, logits, 0.0), axis=0, keepdims=True))
        eb[:, lanes(k)] = logits
    arx[0] = jnp.concatenate([*targets, mix_part[:4]], axis=0)
    for i, p in enumerate(voc_peers):
        net.send(arx.at[0], arx.at[i + 1], ("ar", i), peer(*p))
    onehot = hit.astype(F32)
    for k in range(K):
        eb[:, lanes(k)] = jnp.exp(eb[:, lanes(k)] - ln_ref[k : k + 1, :]) - onehot
    for i in range(len(voc_peers)):
        net.got(arx.at[i + 1], ("ar", i))
    sums = jnp.sum(arx[...], axis=0)
    exp_mix = jnp.exp(sums[4:])
    weights = exp_mix / jnp.sum(exp_mix, axis=0, keepdims=True)
    joint = weights * jnp.exp(sums[:4] - ln_ref[...])
    posterior = joint / jnp.sum(joint, axis=0, keepdims=True)
    factor = loss_ref[...] * posterior
    mix_grad = loss_ref[...] * (weights - posterior)

    for k in ORDER:
        lgt[:, lanes(k)] = (factor[k : k + 1] * eb[:, lanes(k)]).astype(BF)
        net.send(lgt.at[:, lanes(k)], lgp.at[:, lanes(k)], ("lg", k), other)

    net.got(wp, ("wp",))
    w_own = w[:, pl.ds(c, 1)].reshape(8 * E, V)
    for k in ORDER:
        net.got(lgp.at[:, lanes(k)], ("lg", k))
        part = mm(w_own, lgt[:, lanes(k)]) + mm(wp[...].reshape(8 * E, V), lgp[:, lanes(k)])
        cgb[k] = part.astype(BF).reshape(ZL, X, E, T)
        net.send(cgb.at[k, :, xat(2)], r2.at[k], ("r2", k), right if k < 2 else left)
    near = {k: (-1, left, rxp, "rp") if k < 2 else (1, right, rxm, "rm") for k in range(K)}

    def straight(k):
        dx, device, there, role = near[k]
        net.send(cgb.at[k, :, xat(dx)], there.at[k], (role, k), device)

    def combine(k):
        dx, device, there, role = (1, right, rxm, "rm") if k < 2 else (-1, left, rxp, "rp")
        net.got(r2.at[k], ("r2", k))
        sp[k] = (cgb[k, :, xat(dx)].astype(F32) + r2[k].astype(F32)).astype(BF)
        net.send(sp.at[k], there.at[k], (role, k), device)

    straight(0)
    straight(2)

    for a in range(ZH):
        part = mm_nt(ctx[a * 512 : (a + 1) * 512, :], lgt[...])
        vgb[a] = part.astype(BF).reshape(Y, 64, V)
    combine(0)
    combine(2)
    straight(1)
    straight(3)
    combine(1)
    combine(3)
    for dy in (1, 7, 2, 6, 3, 5, 4):
        net.send(vgb.at[:, yat(dy)], vrx.at[dy], ("vy", dy), {"y": yat(dy)})

    def x_done(k):
        net.got(rxm.at[k], ("rm", k))
        net.got(rxp.at[k], ("rp", k))
        xs[k] = cgb[k, :, x].astype(F32) + rxm[k].astype(F32) + rxp[k].astype(F32)
        zs[k] = xs[k, 1 - zl].astype(BF)
        net.send(zs.at[k], zr.at[k], ("zr", k), over)

    def z_done(k):
        net.got(zr.at[k], ("zr", k))
        own = ctx[pl.ds(pl.multiple_of(voc * E, E), E), lanes(k)].astype(F32)
        pre_grad = ((xs[k, zl] + zr[k].astype(F32)) * (1.0 - own * own)).astype(BF)
        pgz[k, :, 0:T] = pre_grad
        pgs[k * E : (k + 1) * E, :] = pre_grad
        net.send(pgz.at[k, :, lanes(0)], pgz.at[k, :, lanes(1)], ("pz", 1, k), {"zh": zat(1)})
        net.send(pgz.at[k, :, lanes(0)], pgz.at[k, :, lanes(3)], ("pz", 3, k), {"zh": zat(3)})

    x_done(0)
    x_done(2)
    for dz in (1, 3, 2):
        net.got(hx.at[dz], ("hx", dz))
    for dz in range(ZH):
        ht[:, lanes(dz)] = hx[dz].T
    z_done(0)
    z_done(2)
    x_done(1)
    x_done(3)
    z_done(1)
    z_done(3)

    for j in range(4):
        part = mm(cp[j * 512 : (j + 1) * 512, :], pgs[...])
        hpb[4 * j : 4 * j + 4] = part.astype(BF).reshape(4, 128, T)

    def far(k):
        net.got(pgz.at[k, :, lanes(1)], ("pz", 1, k))
        if k < 2:
            net.send(pgz.at[k, :, lanes(1)], pgz.at[k, :, lanes(2)], ("pz", 2, k), {"zh": zat(1)})
        net.got(pgz.at[k, :, lanes(3)], ("pz", 3, k))
        if k >= 2:
            net.send(pgz.at[k, :, lanes(3)], pgz.at[k, :, lanes(2)], ("pz", 2, k), {"zh": zat(3)})

    def proj(k):
        net.got(pgz.at[k, :, lanes(2)], ("pz", 2, k))
        pp[k] = mm_nt(ht[...], pgz[k]).astype(BF).reshape(Y, 64, E)
        for dy in (1, 7, 2, 6, 3, 5, 4):
            net.send(pp.at[k, yat(dy)], prx.at[k, dy], ("py", dy, k), {"y": yat(dy)})

    for k in ORDER:
        far(k)
    for i, p in enumerate(voc_peers):
        at = peer(*p)
        net.send(hpb.at[at["zl"] * 8 + at["x"] * 2 + at["c"]], hrx.at[i], ("hr", i), at)
    for k in ORDER:
        proj(k)

    for dy in range(1, Y):
        net.got(vrx.at[dy], ("vy", dy))
    vrx[0] = vgb[:, y]
    total = vrx[0].astype(F32)
    for dy in range(1, Y):
        total = total + vrx[dy].astype(F32)
    vzs[...] = total.astype(BF)
    for dz in (1, 3, 2):
        net.send(vzs.at[zat(dz)], vzr.at[dz], ("vz", dz), {"zh": zat(dz)})

    for i in range(len(voc_peers)):
        net.got(hrx.at[i], ("hr", i))
    total = hpb[voc].astype(F32)
    for i in range(len(voc_peers)):
        total = total + hrx[i].astype(F32)
    mix_grad = jnp.concatenate([mix_grad, jnp.zeros((4, T), F32)], axis=0)
    mix_term = lax.dot_general(mix_grad, mw, TN, precision=lax.Precision.HIGHEST, preferred_element_type=F32)
    hg_ref[...] = (total.T + mix_term).astype(BF)

    for k in ORDER:
        total = pp[k, y].astype(F32)
        for dy in range(1, Y):
            net.got(prx.at[k, dy], ("py", dy, k))
            total = total + prx[k, dy].astype(F32)
        pst[pl.ds(k, 64, stride=K), :] = total
    pg_ref[...] = pst[...].astype(BF)

    total = vzs[zh].astype(F32)
    for dz in range(1, ZH):
        net.got(vzr.at[dz], ("vz", dz))
        total = total + vzr[dz].astype(F32)
    vg_ref[...] = total.astype(BF)
    net.finish()


def body(hidden, mix_weight, comp_proj, vocab_weight, log_normalizer, targets, loss_grad):
    vmem = pl.BlockSpec(memory_space=pltpu.VMEM)
    hbm = pl.BlockSpec(memory_space=pl.ANY)
    scratch = [
        pltpu.VMEM(shape, dtype)
        for shape, dtype in (
            ((T, D), BF),
            ((D * K, E), BF),
            ((D, E), F32),
            ((D, K * E), BF),
            ((8, 2, 128, V), BF),
            ((V, D), BF),
            ((8, 128, V), BF),
            ((D, K * T), BF),
            ((V, K * T), F32),
            ((V, K * T), BF),
            ((V, K * T), BF),
            ((16, 8, T), F32),
            ((K, ZL, X, E, T), BF),
            ((K, ZL, E, T), BF),
            ((K, ZL, E, T), BF),
            ((K, ZL, E, T), BF),
            ((K, ZL, E, T), BF),
            ((K, ZL, E, T), F32),
            ((K, E, T), BF),
            ((K, E, T), BF),
            ((K, E, ZH * T), BF),
            ((K * E, T), BF),
            ((ZH, T, 512), BF),
            ((512, ZH * T), BF),
            ((K, Y, 64, E), BF),
            ((K, Y, 64, E), BF),
            ((64 * K, E), F32),
            ((16, 128, T), BF),
            ((15, 128, T), BF),
            ((ZH, Y, 64, V), BF),
            ((Y, ZH, 64, V), BF),
            ((ZH, 64, V), BF),
            ((ZH, 64, V), BF),
        )
    ]
    scratch += [pltpu.SemaphoreType.DMA((N_SEND,)), pltpu.SemaphoreType.DMA((N_RECV,)), pltpu.SemaphoreType.DMA((8,))]
    hidden_grad, proj_grad, vocab_grad = pl.pallas_call(
        kernel,
        out_shape=(
            jax.ShapeDtypeStruct((T, E), BF),
            jax.ShapeDtypeStruct((64 * K, E), BF),
            jax.ShapeDtypeStruct((64, V), BF),
        ),
        in_specs=[hbm, hbm, hbm, vmem, vmem, vmem, vmem],
        out_specs=(vmem, vmem, vmem),
        scratch_shapes=scratch,
        compiler_params=pltpu.CompilerParams(
            collective_id=0, has_side_effects=True, vmem_limit_bytes=56 * 1024 * 1024
        ),
    )(
        hidden,
        comp_proj.reshape(D * K, E),
        vocab_weight.reshape(8, 2, 128, V),
        mix_weight,
        log_normalizer,
        targets.reshape(1, T),
        loss_grad.reshape(1, T),
    )
    return hidden_grad, proj_grad.reshape(64, K, E), vocab_grad


def solution(mesh):
    split = Mesh(mesh.devices.reshape(ZH, Y, ZL, X, C), ("zh", "y", "zl", "x", "c"))
    tok, voc = ("zh", "y"), ("zl", "x", "c")
    in_specs = (P(tok, None), P(None, voc), P(None, None, voc), P(None, voc), P(None, tok), P(tok), P(tok))
    out_specs = (P(tok, voc), P(tok, None, voc), P(tok, voc))
    return jax.shard_map(body, mesh=split, in_specs=in_specs, out_specs=out_specs, check_vma=False)
```

time: 239 us -> 90 us (0.38)
  the two profiles are of different devices: /device:TPU:1 before, /device:TPU:6 now
where the time goes in v1:
time: 90 us; the launch traced here: 89.7 us
  Pallas kernels  84.8 us (94%)
  local copies, waits for them, and re-layouts  4.24 us (5%)
    pallas_call x1, Pallas kernels, body(): pl.pallas_call(kernel, out_shape=(jax.ShapeDtypeStruct((T, E), BF), jax.S...  84.8 us
    unnamed x3, local copies, waits for them, and re-layouts  4.24 us

profile of v1, /device:TPU:6, one launch (start us, length us, event | category | flops | bytes accessed | tf_op | source)
XLA Modules:
  0.0 89.7 jit_solution(2665342739711734095)
XLA Ops:
  0.6 84.8 %shard_map.94 = (bf16[128,128]{1,0:T(8,128)(2,1)}, bf16[256,128]{1,0:T(8,128)(2,1)}, bf16[64,256]{1,0:T(8,128)(2,1)}) custom-call(bf16[128,2048]{1,0:T(8,128)(2,1)} %hid_hbm.1, bf16[8192,128]{1,0:T(8,128)(2,1)} %bitcast.5, bf16[8,2,128,256]{3,2,1,0:T(8,128)(2,1)} %bitcast.6, bf16[4,128]{1,0:T(4,128)(2,1)} %mw_ref.1, f32[4,128]{1,0:T(4,128)} %ln_ref.1, ...), custom_call_target="tpu_custom_call" | custom-call | tf_op jit(solution)/shard_map/pallas_call | solution.py:375
  85.4 1.4 %copy.13 = bf16[128,128]{1,0:T(8,128)(2,1)} copy(bf16[128,128]{1,0:T(8,128)(2,1)} %get-tuple-element.12) | data formatting | bytes 65536
  86.8 1.5 %copy.14 = bf16[64,4,128]{2,1,0:T(4,128)(2,1)} copy(bf16[64,4,128]{2,1,0:T(4,128)(2,1)} %bitcast.7) | data formatting | bytes 131072
  88.3 1.4 %copy.15 = bf16[64,256]{1,0:T(8,128)(2,1)} copy(bf16[64,256]{1,0:T(8,128)(2,1)} %get-tuple-element.14) | data formatting | bytes 65536

commit v2 on v1

v2 whole, which is shorter than its diff:
```python
import jax
import jax.numpy as jnp
from jax import lax
from jax.experimental import pallas as pl
from jax.experimental.pallas import tpu as pltpu
from jax.sharding import Mesh
from jax.sharding import PartitionSpec as P

MESH = pl.DeviceIdType.MESH
BF, F32 = jnp.bfloat16, jnp.float32
ZH, Y, ZL, X, C = 4, 8, 2, 4, 2
D, K, T, V, E = 2048, 4, 128, 256, 128
N_SEND, N_RECV = 260, 230

NT = (((1,), (1,)), ((), ()))
TN = (((0,), (0,)), ((), ()))


def mm(a, b):
    return jnp.dot(a, b, preferred_element_type=F32)


def mm_nt(a, b):
    return lax.dot_general(a, b, NT, preferred_element_type=F32)


class Net:
    def __init__(self, send_sems, recv_sems):
        self.send_sems, self.recv_sems = send_sems, recv_sems
        self.roles, self.sent = {}, []

    def slot(self, role):
        return self.recv_sems.at[self.roles.setdefault(role, len(self.roles))]

    def send(self, src, dst, role, device):
        copy = pltpu.make_async_remote_copy(
            src_ref=src,
            dst_ref=dst,
            send_sem=self.send_sems.at[len(self.sent)],
            recv_sem=self.slot(role),
            device_id=device,
            device_id_type=MESH,
        )
        copy.start()
        self.sent.append(copy)

    def got(self, dst, role):
        pltpu.make_async_remote_copy(
            src_ref=dst,
            dst_ref=dst,
            send_sem=self.send_sems.at[0],
            recv_sem=self.slot(role),
            device_id={"c": 1 - lax.axis_index("c")},
            device_id_type=MESH,
        ).wait_recv()

    def finish(self):
        for copy in self.sent:
            copy.wait_send()


def kernel(
    hid_hbm, cp_hbm, w_hbm, mw_hbm, ln_hbm, tg_hbm, loss_hbm,
    hg_ref, pg_ref, vg_ref,
    hid, cpraw, stage, cp, w, wt, wp, mw_ref, ln_ref, tg_ref, loss_ref, ctx, eb, lgt, lgp, arx,
    cgb, zf, sf, r2, sp, rxm, rxp, rmo, rpo, zs, zr, pgz, pgs, hx, ht, pp, pc, pn, prx, pst,
    hpb, hrx, vgb, vsb, vrb, vzs, vzr,
    send_sems, recv_sems, local_sems,
):
    zh, y = lax.axis_index("zh"), lax.axis_index("y")
    zl, x, c = lax.axis_index("zl"), lax.axis_index("x"), lax.axis_index("c")
    voc = zl * 8 + x * 2 + c
    net = Net(send_sems, recv_sems)

    def xat(dx):
        return lax.rem(x + dx + X, X)

    def yat(dy):
        return lax.rem(y + dy + Y, Y)

    def zat(dz):
        return lax.rem(zh + dz, ZH)

    def peer(dl, dx, dc):
        return {"zl": (zl + dl) % 2, "x": xat(dx), "c": (c + dc) % 2}

    def lanes(k, n=1):
        return pl.ds(k * T, n * T)

    right, left = {"x": xat(1)}, {"x": xat(-1)}
    up, down = {"y": yat(1)}, {"y": yat(-1)}
    other, over = {"c": 1 - c}, {"zl": 1 - zl}
    voc_peers = [(dl, dx, dc) for dl in range(2) for dx in range(4) for dc in range(2)][1:]

    barrier = pltpu.get_barrier_semaphore()
    greeted = [peer(*p) for p in voc_peers]
    greeted += [{"y": yat(dy)} for dy in (1, 2, 3, 5, 6, 7)] + [{"zh": zat(dz)} for dz in range(1, ZH)]
    parts = 4
    rows = D * K // parts
    loads = [pltpu.make_async_copy(hid_hbm, hid, local_sems.at[0])]
    for q in range(parts):
        span = pl.ds(q * rows, rows)
        loads.append(pltpu.make_async_copy(cp_hbm.at[span], cpraw.at[span], local_sems.at[1 + q]))
    small = [(mw_hbm, mw_ref), (ln_hbm, ln_ref), (tg_hbm, tg_ref), (loss_hbm, loss_ref), (w_hbm, w)]
    for i, (src, dst) in enumerate(small):
        loads.append(pltpu.make_async_copy(src, dst, local_sems.at[1 + parts + i]))
    for load in loads:
        load.start()
    for device in greeted:
        pl.semaphore_signal(barrier, inc=1, device_id=device, device_id_type=MESH)

    loads[0].wait()
    pre = jnp.zeros((T, K * E), F32)
    for q in range(parts):
        loads[1 + q].wait()
        stage[...] = cpraw[pl.ds(q * rows, rows), :].astype(F32)
        span = pl.ds(q * (D // parts), D // parts)
        for k in range(K):
            cp[span, lanes(k)] = stage[pl.ds(k, D // parts, stride=K), :].astype(BF)
        pre = pre + mm(hid[:, span], cp[span, :])
    acts = jnp.tanh(pre)

    def block(dl, dx, dc, k):
        at = (zl + dl) % 2 * 8 + xat(dx) * 2 + (c + dc) % 2
        return ctx.at[pl.ds(pl.multiple_of(at * E, E), E), lanes(k)]

    for k in range(K):
        ctx[pl.ds(pl.multiple_of(voc * E, E), E), lanes(k)] = acts[:, k * E : (k + 1) * E].T.astype(BF)

    pl.semaphore_wait(barrier, len(greeted))

    def push(dl, dx, k, role, device):
        net.send(block(dl, dx, 0, k), block(dl, dx, 0, k), role, device)

    for k in range(K):
        push(0, 0, k, ("ag", 1, 0, k), over)
        push(0, 0, k, ("ag", 0, -1, k), right)
        push(0, 0, k, ("ag", 0, 1, k), left)
        push(0, 0, k, ("ac", 0, 0, k), other)

    def piece(dx, dc):
        return pl.ds(pl.multiple_of((xat(dx) * 2 + (c + dc) % 2) * 16, 16), 16)

    for dz in (1, 3, 2):
        span = pl.ds(pl.multiple_of(zat(dz) * 512, 512), 512)
        net.send(hid.at[piece(0, 0), span], hx.at[dz, piece(0, 0)], ("hx", dz), {"zh": zat(dz)})
    hx[0] = hid[:, pl.ds(pl.multiple_of(zh * 512, 512), 512)]
    for i in range(len(small)):
        loads[1 + parts + i].wait()
    net.send(w.at[:, 1 - c], wp, ("wp",), other)
    mw = jnp.concatenate([mw_ref[...].astype(F32), jnp.zeros((4, E), F32)], axis=0)
    mix_part = mm_nt(mw.astype(BF), hid[:, pl.ds(pl.multiple_of(voc * E, E), E)])
    for j in range(16):
        wt[:, j * 128 : (j + 1) * 128] = w[j // 2, j % 2].T

    def from_side(dl, dx, k):
        net.got(block(dl, dx, 0, k), ("ag", dl, dx, k))
        if dl == 0 and (k % 2 == 0) == (dx == -1):
            push(dl, dx, k, ("ag", 0, 2, k), right if dx == -1 else left)
        push(dl, dx, k, ("ac", dl, dx, k), other)

    def from_far(dl, k):
        net.got(block(dl, 2, 0, k), ("ag", dl, 2, k))
        if dl == 0:
            push(0, 2, k, ("ag", 1, 2, k), over)
        push(dl, 2, k, ("ac", dl, 2, k), other)

    def add_chip(dl, dx):
        for k in range(K):
            net.got(block(dl, dx, 1, k), ("ac", dl, dx, k))
        span = pl.ds(pl.multiple_of(((zl + dl) % 2 * X + xat(dx)) * 256, 256), 256)
        part = mm(wt[:, span], ctx[span, :])
        eb[...] = part if (dl, dx) == (0, 0) else eb[...] + part

    for k in range(K):
        net.got(block(1, 0, 0, k), ("ag", 1, 0, k))
        push(1, 0, k, ("ag", 1, -1, k), right)
        push(1, 0, k, ("ag", 1, 1, k), left)
        push(1, 0, k, ("ac", 1, 0, k), other)
        from_side(0, -1, k)
        from_side(0, 1, k)
    for k, chip in zip(range(K), ((0, 0), (1, 0), (0, -1), (0, 1))):
        from_far(0, k)
        from_side(1, -1, k)
        from_side(1, 1, k)
        add_chip(*chip)
    for k, chip in zip(range(K), ((1, -1), (1, 1), (0, 2), (1, 2))):
        from_far(1, k)
        add_chip(*chip)
    ids = lax.broadcasted_iota(jnp.int32, (V, T), 0) + voc * V
    hit = ids == tg_ref[...]
    targets = [jnp.sum(jnp.where(hit, eb[:, lanes(k)], 0.0), axis=0, keepdims=True) for k in range(K)]
    arx[0] = jnp.concatenate([*targets, mix_part[:4]], axis=0)
    for i, p in enumerate(voc_peers):
        net.send(arx.at[0], arx.at[i + 1], ("ar", i), peer(*p))
    onehot = hit.astype(F32)
    for k in range(K):
        eb[:, lanes(k)] = jnp.exp(eb[:, lanes(k)] - ln_ref[k : k + 1, :]) - onehot
    for i in range(len(voc_peers)):
        net.got(arx.at[i + 1], ("ar", i))
    sums = jnp.sum(arx[...], axis=0)
    exp_mix = jnp.exp(sums[4:])
    weights = exp_mix / jnp.sum(exp_mix, axis=0, keepdims=True)
    joint = weights * jnp.exp(sums[:4] - ln_ref[...])
    posterior = joint / jnp.sum(joint, axis=0, keepdims=True)
    factor = loss_ref[...] * posterior
    mix_grad = loss_ref[...] * (weights - posterior)

    for k in range(K):
        lgt[:, lanes(k)] = (factor[k : k + 1] * eb[:, lanes(k)]).astype(BF)
        net.send(lgt.at[:, lanes(k)], lgp.at[:, lanes(k)], ("lg", k), other)

    for a in range(ZH):
        part = mm_nt(ctx[a * 512 : (a + 1) * 512, :], lgt[...])
        vgb[a] = part.astype(BF).reshape(Y, 64, V)

    def chain_send(way, half, dist):
        sign = 1 - 2 * way
        owner = yat(sign * dist)
        src = vgb.at[2 * half : 2 * half + 2, owner]
        if dist < (4 if half == way else 3):
            got = vrb.at[way, half, dist]
            net.got(got, ("vy", way, half, dist + 1))
            vsb[way, half, dist - 1] = (src[...].astype(F32) + got[...].astype(F32)).astype(BF)
            src = vsb.at[way, half, dist - 1]
        net.send(src, vrb.at[way, half, dist - 1], ("vy", way, half, dist), up if way == 0 else down)

    def chain_round(n):
        for half in range(2):
            for way in range(2):
                dist = (4 if half == way else 3) - n
                if dist > 0:
                    chain_send(way, half, dist)

    chain_round(0)

    net.got(wp, ("wp",))
    w_own = w[:, pl.ds(c, 1)].reshape(8 * E, V)
    for k in (0, 2):
        net.got(lgp.at[:, lanes(k)], ("lg", k))
        net.got(lgp.at[:, lanes(k + 1)], ("lg", k + 1))
        part = mm(w_own, lgt[:, lanes(k, 2)]) + mm(wp[...].reshape(8 * E, V), lgp[:, lanes(k, 2)])
        for j in (k, k + 1):
            cgb[j] = part[:, (j - k) * T : (j - k + 1) * T].astype(BF).reshape(ZL, X, E, T)
        for j in (k, k + 1):
            net.send(cgb.at[j, 1 - zl, xat(2)], zf.at[j], ("zf", j), over)
            net.send(cgb.at[j, 1 - zl, xat(1)], rmo.at[j], ("rmo", j), right)
            net.send(cgb.at[j, 1 - zl, xat(-1)], rpo.at[j], ("rpo", j), left)

    def both(a, b):
        return (a[...].astype(F32) + b[...].astype(F32)).astype(BF)

    def far(k):
        net.got(zf.at[k], ("zf", k))
        sf[k] = both(cgb.at[k, zl, xat(2)], zf.at[k])
        net.send(sf.at[k], r2.at[k], ("r2", k), left if k % 2 else right)

    def straight(k):
        if k % 2:
            net.send(cgb.at[k, zl, xat(1)], rxm.at[k], ("rm", k), right)
        else:
            net.send(cgb.at[k, zl, xat(-1)], rxp.at[k], ("rp", k), left)

    def combine(k):
        net.got(r2.at[k], ("r2", k))
        sp[k] = both(cgb.at[k, zl, xat(-1 if k % 2 else 1)], r2.at[k])
        if k % 2:
            net.send(sp.at[k], rxp.at[k], ("rp", k), left)
        else:
            net.send(sp.at[k], rxm.at[k], ("rm", k), right)

    def cross(k):
        net.got(rmo.at[k], ("rmo", k))
        net.got(rpo.at[k], ("rpo", k))
        zs[k] = (cgb[k, 1 - zl, x].astype(F32) + rmo[k].astype(F32) + rpo[k].astype(F32)).astype(BF)
        net.send(zs.at[k], zr.at[k], ("zr", k), over)

    far(0)
    far(1)
    straight(0)
    straight(1)
    far(2)
    far(3)
    straight(2)
    straight(3)
    cross(0)
    cross(1)
    combine(0)
    combine(1)
    cross(2)
    cross(3)
    combine(2)
    combine(3)
    chain_round(1)

    def pre_grads(k):
        net.got(rxm.at[k], ("rm", k))
        net.got(rxp.at[k], ("rp", k))
        net.got(zr.at[k], ("zr", k))
        own = ctx[pl.ds(pl.multiple_of(voc * E, E), E), lanes(k)].astype(F32)
        grad = cgb[k, zl, x].astype(F32) + rxm[k].astype(F32) + rxp[k].astype(F32) + zr[k].astype(F32)
        grad = (grad * (1.0 - own * own)).astype(BF)
        pgz[k, :, 0:T] = grad
        pgs[k * E : (k + 1) * E, :] = grad
        net.send(pgz.at[k, :, lanes(0)], pgz.at[k, :, lanes(1)], ("pz", 1, k), {"zh": zat(1)})
        net.send(pgz.at[k, :, lanes(0)], pgz.at[k, :, lanes(3)], ("pz", 3, k), {"zh": zat(3)})

    pre_grads(0)
    pre_grads(1)
    pre_grads(2)
    pre_grads(3)

    for dz in (1, 3, 2):
        net.got(hx.at[dz, piece(0, 0)], ("hx", dz))
    row_peers = [(dx, dc) for dx in (1, 3, 2, 0) for dc in range(2) if (dx, dc) != (0, 0)]
    for dx, dc in row_peers:
        at = {"x": xat(dx), "c": (c + dc) % 2}
        net.send(hx.at[1:4, piece(0, 0)], hx.at[1:4, piece(0, 0)], ("hy", (4 - dx) % 4, dc), at)

    for j in range(4):
        part = mm(cp[j * 512 : (j + 1) * 512, :], pgs[...])
        hpb[4 * j : 4 * j + 4] = part.astype(BF).reshape(4, 128, T)
    chain_round(2)

    for k in range(K):
        net.got(pgz.at[k, :, lanes(1)], ("pz", 1, k))
        if k % 2 == 0:
            net.send(pgz.at[k, :, lanes(1)], pgz.at[k, :, lanes(2)], ("pz", 2, k), {"zh": zat(1)})
        net.got(pgz.at[k, :, lanes(3)], ("pz", 3, k))
        if k % 2 == 1:
            net.send(pgz.at[k, :, lanes(3)], pgz.at[k, :, lanes(2)], ("pz", 2, k), {"zh": zat(3)})
    for i, p in enumerate(voc_peers):
        at = peer(*p)
        net.send(hpb.at[at["zl"] * 8 + at["x"] * 2 + at["c"]], hrx.at[i], ("hr", i), at)
    for dx, dc in row_peers:
        net.got(hx.at[1:4, piece(dx, dc)], ("hy", dx, dc))
    for dz in range(ZH):
        ht[:, lanes(dz)] = hx[dz].T

    def proj(k):
        for j in (k, k + 1):
            net.got(pgz.at[j, :, lanes(2)], ("pz", 2, j))
        part = mm_nt(ht[...], pgz[k : k + 2].reshape(2 * E, ZH * T))
        for j in (k, k + 1):
            pp[j] = part[:, (j - k) * E : (j - k + 1) * E].astype(BF).reshape(Y, 64, E)
        for j in (k, k + 1):
            sign, far_way, near_way = (-1, down, up) if j % 2 else (1, up, down)
            net.send(pp.at[j, yat(4 * sign)], pn.at[j, 0], ("pn", j, 0), far_way)
            net.send(pp.at[j, yat(2 * sign)], pn.at[j, 1], ("pn", j, 1), far_way)
            net.send(pp.at[j, yat(-3 * sign)], pn.at[j, 2], ("pn", j, 2), near_way)
            net.send(pp.at[j, yat(-sign)], prx.at[j, 3], ("py", j, 3), near_way)

    def proj_on(j):
        sign = -1 if j % 2 else 1
        for i, dist in enumerate((3 * sign, sign, -2 * sign)):
            net.got(pn.at[j, i], ("pn", j, i))
            pc[j, i] = both(pp.at[j, yat(dist)], pn.at[j, i])
            net.send(pc.at[j, i], prx.at[j, i], ("py", j, i), {"y": yat(dist)})

    proj(0)
    proj(2)
    chain_round(3)
    for k in range(K):
        proj_on(k)

    for half in range(2):
        span = slice(2 * half, 2 * half + 2)
        total = vgb[span, y].astype(F32)
        for way in range(2):
            net.got(vrb.at[way, half, 0], ("vy", way, half, 1))
            total = total + vrb[way, half, 0].astype(F32)
        vzs[span] = total.astype(BF)
    for dz in (1, 3, 2):
        net.send(vzs.at[zat(dz)], vzr.at[dz], ("vz", dz), {"zh": zat(dz)})

    for i in range(len(voc_peers)):
        net.got(hrx.at[i], ("hr", i))
    total = hpb[voc].astype(F32)
    for i in range(len(voc_peers)):
        total = total + hrx[i].astype(F32)
    mix_grad = jnp.concatenate([mix_grad, jnp.zeros((4, T), F32)], axis=0)
    mix_term = lax.dot_general(mix_grad, mw, TN, precision=lax.Precision.HIGHEST, preferred_element_type=F32)
    hg_ref[...] = (total.T + mix_term).astype(BF)

    for k in range(K):
        total = pp[k, y].astype(F32)
        for i in range(4):
            net.got(prx.at[k, i], ("py", k, i))
            total = total + prx[k, i].astype(F32)
        pst[pl.ds(k, 64, stride=K), :] = total
    pg_ref[...] = pst[...].astype(BF)

    total = vzs[zh].astype(F32)
    for dz in range(1, ZH):
        net.got(vzr.at[dz], ("vz", dz))
        total = total + vzr[dz].astype(F32)
    vg_ref[...] = total.astype(BF)
    net.finish()


def hand_over(*refs):
    for src, dst in zip(refs[:3], refs[3:]):
        dst[...] = src[...]


def body(hidden, mix_weight, comp_proj, vocab_weight, log_normalizer, targets, loss_grad):
    vmem = pl.BlockSpec(memory_space=pltpu.VMEM)
    hbm = pl.BlockSpec(memory_space=pl.ANY)
    scratch = [
        pltpu.VMEM(shape, dtype)
        for shape, dtype in (
            ((T, D), BF),
            ((D * K, E), BF),
            ((D, E), F32),
            ((D, K * E), BF),
            ((8, 2, 128, V), BF),
            ((V, D), BF),
            ((8, 128, V), BF),
            ((K, E), BF),
            ((K, T), F32),
            ((1, T), jnp.int32),
            ((1, T), F32),
            ((D, K * T), BF),
            ((V, K * T), F32),
            ((V, K * T), BF),
            ((V, K * T), BF),
            ((16, 8, T), F32),
            ((K, ZL, X, E, T), BF),
            *[((K, E, T), BF)] * 10,
            ((K, E, ZH * T), BF),
            ((K * E, T), BF),
            ((ZH, T, 512), BF),
            ((512, ZH * T), BF),
            ((K, Y, 64, E), BF),
            ((K, 3, 64, E), BF),
            ((K, 3, 64, E), BF),
            ((K, 4, 64, E), BF),
            ((64 * K, E), F32),
            ((16, 128, T), BF),
            ((15, 128, T), BF),
            ((ZH, Y, 64, V), BF),
            ((2, 2, 4, 2, 64, V), BF),
            ((2, 2, 4, 2, 64, V), BF),
            ((ZH, 64, V), BF),
            ((ZH, 64, V), BF),
        )
    ]
    scratch += [pltpu.SemaphoreType.DMA((N_SEND,)), pltpu.SemaphoreType.DMA((N_RECV,)), pltpu.SemaphoreType.DMA((10,))]
    shapes = (
        jax.ShapeDtypeStruct((T, E), BF),
        jax.ShapeDtypeStruct((64 * K, E), BF),
        jax.ShapeDtypeStruct((64, V), BF),
    )
    results = pl.pallas_call(
        kernel,
        out_shape=shapes,
        in_specs=[hbm] * 7,
        out_specs=(vmem, vmem, vmem),
        scratch_shapes=scratch,
        compiler_params=pltpu.CompilerParams(
            collective_id=0, has_side_effects=True, vmem_limit_bytes=56 * 1024 * 1024
        ),
    )(
        hidden,
        comp_proj.reshape(D * K, E),
        vocab_weight.reshape(8, 2, 128, V),
        mix_weight,
        log_normalizer,
        targets.reshape(1, T),
        loss_grad.reshape(1, T),
    )
    hidden_grad, proj_grad, vocab_grad = pl.pallas_call(
        hand_over, out_shape=shapes, in_specs=[vmem] * 3, out_specs=(vmem,) * 3
    )(*results)
    return hidden_grad, proj_grad.reshape(64, K, E), vocab_grad


def solution(mesh):
    split = Mesh(mesh.devices.reshape(ZH, Y, ZL, X, C), ("zh", "y", "zl", "x", "c"))
    tok, voc = ("zh", "y"), ("zl", "x", "c")
    in_specs = (P(tok, None), P(None, voc), P(None, None, voc), P(None, voc), P(None, tok), P(tok), P(tok))
    out_specs = (P(tok, voc), P(tok, None, voc), P(tok, voc))
    return jax.shard_map(body, mesh=split, in_specs=in_specs, out_specs=out_specs, check_vma=False)
```

time: 90 us -> 74.3 us (0.83)
  the two profiles are of different devices: /device:TPU:6 before, /device:TPU:64 now
where the time goes in v2:
time: 74.3 us; the launch traced here: 74.1 us
  Pallas kernels  73.5 us (99%)
    pallas_call x1, Pallas kernels, body(): pl.pallas_call(kernel, out_shape=shapes, in_specs=[hbm] * 7, out_specs=(v...  72 us
    pallas_call x1, Pallas kernels, body(): pl.pallas_call(hand_over, out_shape=shapes, in_specs=[vmem] * 3, out_spec...  1.49 us

profile of v2, /device:TPU:64, one launch (start us, length us, event | category | flops | bytes accessed | tf_op | source)
XLA Modules:
  0.0 74.1 jit_solution(10199053433965781153)
XLA Ops:
  0.6 72.0 %shard_map.94 = (bf16[128,128]{1,0:T(8,128)(2,1)}, bf16[256,128]{1,0:T(8,128)(2,1)}, bf16[64,256]{1,0:T(8,128)(2,1)}) custom-call(bf16[128,2048]{1,0:T(8,128)(2,1)} %hid_hbm.1, bf16[8192,128]{1,0:T(8,128)(2,1)} %bitcast.5, bf16[8,2,128,256]{3,2,1,0:T(8,128)(2,1)} %bitcast.6, bf16[4,128]{1,0:T(4,128)(2,1)} %mw_hbm.1, f32[4,128]{1,0:T(4,128)} %ln_hbm.1, ...), custom_call_target="tpu_custom_call" | custom-call | tf_op jit(solution)/shard_map/pallas_call | solution.py:454
  72.6 1.5 %shard_map.95 = (bf16[128,128]{1,0:T(8,128)(2,1)}, bf16[256,128]{1,0:T(8,128)(2,1)}, bf16[64,256]{1,0:T(8,128)(2,1)}) custom-call(bf16[128,128]{1,0:T(8,128)(2,1)} %get-tuple-element.9.refs_0_, bf16[256,128]{1,0:T(8,128)(2,1)} %get-tuple-element.10.refs_1_, bf16[64,256]{1,0:T(8,128)(2,1)} %get-tuple-element.11.refs_2_), custom_call_target="tpu_custom_call" | custom-call | tf_op jit(solution)/shard_map/pallas_call | solution.py:472

commit v3 on v2

--- a/solution.py
+++ b/solution.py
@@ -1,3 +1,5 @@
+import math
+
 import jax
 import jax.numpy as jnp
 from jax import lax
@@ -10,7 +12,8 @@
 BF, F32 = jnp.bfloat16, jnp.float32
 ZH, Y, ZL, X, C = 4, 8, 2, 4, 2
 D, K, T, V, E = 2048, 4, 128, 256, 128
-N_SEND, N_RECV = 260, 230
+BULK = 2 * 1024 * 1024
+N_SEND, N_RECV = 4, 102
 
 NT = (((1,), (1,)), ((), ()))
 TN = (((0,), (0,)), ((), ()))
@@ -25,52 +28,51 @@
 
 
 class Net:
-    def __init__(self, send_sems, recv_sems):
-        self.send_sems, self.recv_sems = send_sems, recv_sems
-        self.roles, self.sent = {}, []
+    def __init__(self, send_sems, recv_sems, yard):
+        self.send_sems, self.recv_sems, self.yard = send_sems, recv_sems, yard
+        self.roles, self.bulk = {}, []
 
     def slot(self, role):
         return self.recv_sems.at[self.roles.setdefault(role, len(self.roles))]
 
-    def send(self, src, dst, role, device):
-        copy = pltpu.make_async_remote_copy(
+    def copy(self, src, dst, role, device):
+        return pltpu.make_async_remote_copy(
             src_ref=src,
             dst_ref=dst,
-            send_sem=self.send_sems.at[len(self.sent)],
+            send_sem=self.send_sems.at[max(len(self.bulk), 1) - 1],
             recv_sem=self.slot(role),
             device_id=device,
             device_id_type=MESH,
         )
-        copy.start()
-        self.sent.append(copy)
+
+    def send(self, src, dst, role, device):
+        size = math.prod(src.shape) * src.dtype.itemsize
+        if not self.bulk or self.bulk[-1] + size > BULK:
+            self.bulk.append(0)
+        self.bulk[-1] += size
+        self.copy(src, dst, role, device).start()
 
     def got(self, dst, role):
-        pltpu.make_async_remote_copy(
-            src_ref=dst,
-            dst_ref=dst,
-            send_sem=self.send_sems.at[0],
-            recv_sem=self.slot(role),
-            device_id={"c": 1 - lax.axis_index("c")},
-            device_id_type=MESH,
-        ).wait_recv()
+        self.copy(dst, dst, role, {"c": 1 - lax.axis_index("c")}).wait_recv()
 
     def finish(self):
-        for copy in self.sent:
-            copy.wait_send()
+        for i, size in enumerate(self.bulk):
+            sent = self.yard.at[pl.ds(0, size // (E * 2))]
+            pltpu.make_async_copy(sent, sent, self.send_sems.at[i]).wait()
 
 
 def kernel(
     hid_hbm, cp_hbm, w_hbm, mw_hbm, ln_hbm, tg_hbm, loss_hbm,
     hg_ref, pg_ref, vg_ref,
     hid, cpraw, stage, cp, w, wt, wp, mw_ref, ln_ref, tg_ref, loss_ref, ctx, eb, lgt, lgp, arx,
-    cgb, zf, sf, r2, sp, rxm, rxp, rmo, rpo, zs, zr, pgz, pgs, hx, ht, pp, pc, pn, prx, pst,
-    hpb, hrx, vgb, vsb, vrb, vzs, vzr,
+    cgb, zf, sf, r2, sp, zs, rx, ro, pgz, pgs, hx, ht, pp, pc, pn, prx, pst,
+    hpb, hq, hs, hrx, hsum, hz, hzr, vgb, vsb, vrb, vzs, vzr,
     send_sems, recv_sems, local_sems,
 ):
     zh, y = lax.axis_index("zh"), lax.axis_index("y")
     zl, x, c = lax.axis_index("zl"), lax.axis_index("x"), lax.axis_index("c")
     voc = zl * 8 + x * 2 + c
-    net = Net(send_sems, recv_sems)
+    net = Net(send_sems, recv_sems, cpraw)
 
     def xat(dx):
         return lax.rem(x + dx + X, X)
@@ -132,18 +134,18 @@
     def push(dl, dx, k, role, device):
         net.send(block(dl, dx, 0, k), block(dl, dx, 0, k), role, device)
 
-    for k in range(K):
+    for k, to_right, to_left in zip(range(K), (0, 2, 1, 3), (1, 3, 0, 2)):
+        push(0, 0, to_right, ("ag", 0, -1, to_right), right)
+        push(0, 0, to_left, ("ag", 0, 1, to_left), left)
         push(0, 0, k, ("ag", 1, 0, k), over)
-        push(0, 0, k, ("ag", 0, -1, k), right)
-        push(0, 0, k, ("ag", 0, 1, k), left)
-        push(0, 0, k, ("ac", 0, 0, k), other)
+        push(0, 0, k, ("ac", 0, 0), other)
 
     def piece(dx, dc):
         return pl.ds(pl.multiple_of((xat(dx) * 2 + (c + dc) % 2) * 16, 16), 16)
 
     for dz in (1, 3, 2):
         span = pl.ds(pl.multiple_of(zat(dz) * 512, 512), 512)
-        net.send(hid.at[piece(0, 0), span], hx.at[dz, piece(0, 0)], ("hx", dz), {"zh": zat(dz)})
+        net.send(hid.at[piece(0, 0), span], hx.at[dz, piece(0, 0)], ("hx",), {"zh": zat(dz)})
     hx[0] = hid[:, pl.ds(pl.multiple_of(zh * 512, 512), 512)]
     for i in range(len(small)):
         loads[1 + parts + i].wait()
@@ -157,47 +159,51 @@
         net.got(block(dl, dx, 0, k), ("ag", dl, dx, k))
         if dl == 0 and (k % 2 == 0) == (dx == -1):
             push(dl, dx, k, ("ag", 0, 2, k), right if dx == -1 else left)
-        push(dl, dx, k, ("ac", dl, dx, k), other)
+        push(dl, dx, k, ("ac", dl, dx), other)
 
     def from_far(dl, k):
         net.got(block(dl, 2, 0, k), ("ag", dl, 2, k))
         if dl == 0:
             push(0, 2, k, ("ag", 1, 2, k), over)
-        push(dl, 2, k, ("ac", dl, 2, k), other)
+        push(dl, 2, k, ("ac", dl, 2), other)
 
     def add_chip(dl, dx):
-        for k in range(K):
-            net.got(block(dl, dx, 1, k), ("ac", dl, dx, k))
+        at = (zl + dl) % 2 * 8 + xat(dx) * 2 + 1 - c
+        net.got(ctx.at[pl.ds(pl.multiple_of(at * E, E), E)], ("ac", dl, dx))
         span = pl.ds(pl.multiple_of(((zl + dl) % 2 * X + xat(dx)) * 256, 256), 256)
         part = mm(wt[:, span], ctx[span, :])
         eb[...] = part if (dl, dx) == (0, 0) else eb[...] + part
 
+    for dx, k in ((-1, 0), (1, 1), (-1, 2), (1, 3)):
+        from_side(0, dx, k)
     for k in range(K):
         net.got(block(1, 0, 0, k), ("ag", 1, 0, k))
         push(1, 0, k, ("ag", 1, -1, k), right)
         push(1, 0, k, ("ag", 1, 1, k), left)
-        push(1, 0, k, ("ac", 1, 0, k), other)
-        from_side(0, -1, k)
-        from_side(0, 1, k)
-    for k, chip in zip(range(K), ((0, 0), (1, 0), (0, -1), (0, 1))):
+        push(1, 0, k, ("ac", 1, 0), other)
+    for dx, k in ((-1, 1), (1, 0), (-1, 3), (1, 2)):
+        from_side(0, dx, k)
+    add_chip(0, 0)
+    for k in range(K):
         from_far(0, k)
+    for k, chip in zip(range(K), ((1, 0), (0, -1), (0, 1), (0, 2))):
         from_side(1, -1, k)
         from_side(1, 1, k)
         add_chip(*chip)
-    for k, chip in zip(range(K), ((1, -1), (1, 1), (0, 2), (1, 2))):
+    for k in range(K):
         from_far(1, k)
+    for chip in ((1, -1), (1, 1), (1, 2)):
         add_chip(*chip)
     ids = lax.broadcasted_iota(jnp.int32, (V, T), 0) + voc * V
     hit = ids == tg_ref[...]
     targets = [jnp.sum(jnp.where(hit, eb[:, lanes(k)], 0.0), axis=0, keepdims=True) for k in range(K)]
     arx[0] = jnp.concatenate([*targets, mix_part[:4]], axis=0)
     for i, p in enumerate(voc_peers):
-        net.send(arx.at[0], arx.at[i + 1], ("ar", i), peer(*p))
+        net.send(arx.at[0], arx.at[i + 1], ("ar",), peer(*p))
     onehot = hit.astype(F32)
     for k in range(K):
         eb[:, lanes(k)] = jnp.exp(eb[:, lanes(k)] - ln_ref[k : k + 1, :]) - onehot
-    for i in range(len(voc_peers)):
-        net.got(arx.at[i + 1], ("ar", i))
+    net.got(arx.at[1:16], ("ar",))
     sums = jnp.sum(arx[...], axis=0)
     exp_mix = jnp.exp(sums[4:])
     weights = exp_mix / jnp.sum(exp_mix, axis=0, keepdims=True)
@@ -208,7 +214,8 @@
 
     for k in range(K):
         lgt[:, lanes(k)] = (factor[k : k + 1] * eb[:, lanes(k)]).astype(BF)
-        net.send(lgt.at[:, lanes(k)], lgp.at[:, lanes(k)], ("lg", k), other)
+        if k % 2:
+            net.send(lgt.at[:, lanes(k - 1, 2)], lgp.at[:, lanes(k - 1, 2)], ("lg", k - 1), other)
 
     for a in range(ZH):
         part = mm_nt(ctx[a * 512 : (a + 1) * 512, :], lgt[...])
@@ -237,15 +244,14 @@
     net.got(wp, ("wp",))
     w_own = w[:, pl.ds(c, 1)].reshape(8 * E, V)
     for k in (0, 2):
-        net.got(lgp.at[:, lanes(k)], ("lg", k))
-        net.got(lgp.at[:, lanes(k + 1)], ("lg", k + 1))
+        net.got(lgp.at[:, lanes(k, 2)], ("lg", k))
         part = mm(w_own, lgt[:, lanes(k, 2)]) + mm(wp[...].reshape(8 * E, V), lgp[:, lanes(k, 2)])
         for j in (k, k + 1):
             cgb[j] = part[:, (j - k) * T : (j - k + 1) * T].astype(BF).reshape(ZL, X, E, T)
         for j in (k, k + 1):
             net.send(cgb.at[j, 1 - zl, xat(2)], zf.at[j], ("zf", j), over)
-            net.send(cgb.at[j, 1 - zl, xat(1)], rmo.at[j], ("rmo", j), right)
-            net.send(cgb.at[j, 1 - zl, xat(-1)], rpo.at[j], ("rpo", j), left)
+            net.send(cgb.at[j, 1 - zl, xat(1)], ro.at[j, 0], ("ro", j), right)
+            net.send(cgb.at[j, 1 - zl, xat(-1)], ro.at[j, 1], ("ro", j), left)
 
     def both(a, b):
         return (a[...].astype(F32) + b[...].astype(F32)).astype(BF)
@@ -257,23 +263,22 @@
 
     def straight(k):
         if k % 2:
-            net.send(cgb.at[k, zl, xat(1)], rxm.at[k], ("rm", k), right)
+            net.send(cgb.at[k, zl, xat(1)], rx.at[k, 0], ("rx", k), right)
         else:
-            net.send(cgb.at[k, zl, xat(-1)], rxp.at[k], ("rp", k), left)
+            net.send(cgb.at[k, zl, xat(-1)], rx.at[k, 1], ("rx", k), left)
 
     def combine(k):
         net.got(r2.at[k], ("r2", k))
         sp[k] = both(cgb.at[k, zl, xat(-1 if k % 2 else 1)], r2.at[k])
         if k % 2:
-            net.send(sp.at[k], rxp.at[k], ("rp", k), left)
+            net.send(sp.at[k], rx.at[k, 1], ("rx", k), left)
         else:
-            net.send(sp.at[k], rxm.at[k], ("rm", k), right)
+            net.send(sp.at[k], rx.at[k, 0], ("rx", k), right)
 
     def cross(k):
-        net.got(rmo.at[k], ("rmo", k))
-        net.got(rpo.at[k], ("rpo", k))
-        zs[k] = (cgb[k, 1 - zl, x].astype(F32) + rmo[k].astype(F32) + rpo[k].astype(F32)).astype(BF)
-        net.send(zs.at[k], zr.at[k], ("zr", k), over)
+        net.got(ro.at[k], ("ro", k))
+        zs[k] = (cgb[k, 1 - zl, x].astype(F32) + ro[k, 0].astype(F32) + ro[k, 1].astype(F32)).astype(BF)
+        net.send(zs.at[k], rx.at[k, 2], ("rx", k), over)
 
     far(0)
     far(1)
@@ -294,11 +299,9 @@
     chain_round(1)
 
     def pre_grads(k):
-        net.got(rxm.at[k], ("rm", k))
-        net.got(rxp.at[k], ("rp", k))
-        net.got(zr.at[k], ("zr", k))
+        net.got(rx.at[k], ("rx", k))
         own = ctx[pl.ds(pl.multiple_of(voc * E, E), E), lanes(k)].astype(F32)
-        grad = cgb[k, zl, x].astype(F32) + rxm[k].astype(F32) + rxp[k].astype(F32) + zr[k].astype(F32)
+        grad = cgb[k, zl, x].astype(F32) + rx[k, 0].astype(F32) + rx[k, 1].astype(F32) + rx[k, 2].astype(F32)
         grad = (grad * (1.0 - own * own)).astype(BF)
         pgz[k, :, 0:T] = grad
         pgs[k * E : (k + 1) * E, :] = grad
@@ -310,8 +313,7 @@
     pre_grads(2)
     pre_grads(3)
 
-    for dz in (1, 3, 2):
-        net.got(hx.at[dz, piece(0, 0)], ("hx", dz))
+    net.got(hx.at[1:4, piece(0, 0)], ("hx",))
     row_peers = [(dx, dc) for dx in (1, 3, 2, 0) for dc in range(2) if (dx, dc) != (0, 0)]
     for dx, dc in row_peers:
         at = {"x": xat(dx), "c": (c + dc) % 2}
@@ -319,19 +321,26 @@
 
     for j in range(4):
         part = mm(cp[j * 512 : (j + 1) * 512, :], pgs[...])
-        hpb[4 * j : 4 * j + 4] = part.astype(BF).reshape(4, 128, T)
+        hpb[2 * j : 2 * j + 2] = part.astype(BF).reshape(2, 2, 128, T)
+    net.send(hpb.at[:, 1 - c], hq, ("hq",), other)
     chain_round(2)
 
-    for k in range(K):
+    def z_forward(k):
         net.got(pgz.at[k, :, lanes(1)], ("pz", 1, k))
         if k % 2 == 0:
             net.send(pgz.at[k, :, lanes(1)], pgz.at[k, :, lanes(2)], ("pz", 2, k), {"zh": zat(1)})
         net.got(pgz.at[k, :, lanes(3)], ("pz", 3, k))
         if k % 2 == 1:
             net.send(pgz.at[k, :, lanes(3)], pgz.at[k, :, lanes(2)], ("pz", 2, k), {"zh": zat(3)})
-    for i, p in enumerate(voc_peers):
-        at = peer(*p)
-        net.send(hpb.at[at["zl"] * 8 + at["x"] * 2 + at["c"]], hrx.at[i], ("hr", i), at)
+
+    net.got(hq, ("hq",))
+    for j in range(8):
+        hs[j // X, j % X] = both(hpb.at[j, c], hq.at[j])
+    for dx in (1, 3, 2):
+        net.send(hs.at[:, xat(dx)], hrx.at[dx - 1], ("hr",), {"x": xat(dx)})
+    for k in range(K):
+        z_forward(k)
+    chain_round(3)
     for dx, dc in row_peers:
         net.got(hx.at[1:4, piece(dx, dc)], ("hy", dx, dc))
     for dz in range(ZH):
@@ -345,23 +354,20 @@
             pp[j] = part[:, (j - k) * E : (j - k + 1) * E].astype(BF).reshape(Y, 64, E)
         for j in (k, k + 1):
             sign, far_way, near_way = (-1, down, up) if j % 2 else (1, up, down)
-            net.send(pp.at[j, yat(4 * sign)], pn.at[j, 0], ("pn", j, 0), far_way)
-            net.send(pp.at[j, yat(2 * sign)], pn.at[j, 1], ("pn", j, 1), far_way)
-            net.send(pp.at[j, yat(-3 * sign)], pn.at[j, 2], ("pn", j, 2), near_way)
-            net.send(pp.at[j, yat(-sign)], prx.at[j, 3], ("py", j, 3), near_way)
+            net.send(pp.at[j, yat(4 * sign)], pn.at[j, 0], ("pn", j), far_way)
+            net.send(pp.at[j, yat(2 * sign)], pn.at[j, 1], ("pn", j), far_way)
+            net.send(pp.at[j, yat(-3 * sign)], pn.at[j, 2], ("pn", j), near_way)
+            net.send(pp.at[j, yat(-sign)], prx.at[j, 3], ("py", j), near_way)
 
     def proj_on(j):
         sign = -1 if j % 2 else 1
+        net.got(pn.at[j], ("pn", j))
         for i, dist in enumerate((3 * sign, sign, -2 * sign)):
-            net.got(pn.at[j, i], ("pn", j, i))
             pc[j, i] = both(pp.at[j, yat(dist)], pn.at[j, i])
-            net.send(pc.at[j, i], prx.at[j, i], ("py", j, i), {"y": yat(dist)})
+            net.send(pc.at[j, i], prx.at[j, i], ("py", j), {"y": yat(dist)})
 
     proj(0)
     proj(2)
-    chain_round(3)
-    for k in range(K):
-        proj_on(k)
 
     for half in range(2):
         span = slice(2 * half, 2 * half + 2)
@@ -371,31 +377,37 @@
             total = total + vrb[way, half, 0].astype(F32)
         vzs[span] = total.astype(BF)
     for dz in (1, 3, 2):
-        net.send(vzs.at[zat(dz)], vzr.at[dz], ("vz", dz), {"zh": zat(dz)})
-
-    for i in range(len(voc_peers)):
-        net.got(hrx.at[i], ("hr", i))
-    total = hpb[voc].astype(F32)
-    for i in range(len(voc_peers)):
-        total = total + hrx[i].astype(F32)
+        net.send(vzs.at[zat(dz)], vzr.at[dz], ("vz",), {"zh": zat(dz)})
+    for k in range(K):
+        proj_on(k)
+    net.got(hrx, ("hr",))
+    hsum[...] = hs[:, x].astype(F32)
+    for i in range(3):
+        hsum[...] += hrx[i].astype(F32)
+    hz[...] = hsum[1 - zl].astype(BF)
+    net.send(hz, hzr, ("hz",), over)
+
+    for k in range(K):
+        net.got(prx.at[k], ("py", k))
+        total = pp[k, y].astype(F32)
+        for i in range(4):
+            total = total + prx[k, i].astype(F32)
+        pst[pl.ds(k, 64, stride=K), :] = total
+    pg_ref[...] = pst[...].astype(BF)
+
+    net.got(hzr, ("hz",))
+    total = hsum[zl] + hzr[...].astype(F32)
     mix_grad = jnp.concatenate([mix_grad, jnp.zeros((4, T), F32)], axis=0)
     mix_term = lax.dot_general(mix_grad, mw, TN, precision=lax.Precision.HIGHEST, preferred_element_type=F32)
     hg_ref[...] = (total.T + mix_term).astype(BF)
 
-    for k in range(K):
-        total = pp[k, y].astype(F32)
-        for i in range(4):
-            net.got(prx.at[k, i], ("py", k, i))
-            total = total + prx[k, i].astype(F32)
-        pst[pl.ds(k, 64, stride=K), :] = total
-    pg_ref[...] = pst[...].astype(BF)
-
     total = vzs[zh].astype(F32)
+    net.got(vzr.at[1:4], ("vz",))
     for dz in range(1, ZH):
-        net.got(vzr.at[dz], ("vz", dz))
         total = total + vzr[dz].astype(F32)
     vg_ref[...] = total.astype(BF)
     net.finish()
+    assert len(net.bulk) <= N_SEND and len(net.roles) <= N_RECV
 
 
 def hand_over(*refs):
@@ -426,7 +438,9 @@
             ((V, K * T), BF),
             ((16, 8, T), F32),
             ((K, ZL, X, E, T), BF),
-            *[((K, E, T), BF)] * 10,
+            *[((K, E, T), BF)] * 5,
+            ((K, 3, E, T), BF),
+            ((K, 2, E, T), BF),
             ((K, E, ZH * T), BF),
             ((K * E, T), BF),
             ((ZH, T, 512), BF),
@@ -436,8 +450,13 @@
             ((K, 3, 64, E), BF),
             ((K, 4, 64, E), BF),
             ((64 * K, E), F32),
-            ((16, 128, T), BF),
-            ((15, 128, T), BF),
+            ((8, 2, 128, T), BF),
+            ((8, 128, T), BF),
+            ((ZL, X, 128, T), BF),
+            ((3, ZL, 128, T), BF),
+            ((ZL, 128, T), F32),
+            ((128, T), BF),
+            ((128, T), BF),
             ((ZH, Y, 64, V), BF),
             ((2, 2, 4, 2, 64, V), BF),
             ((2, 2, 4, 2, 64, V), BF),

time: 74.3 us -> 66.6 us (0.90)
  the two profiles are of different devices: /device:TPU:64 before, /device:TPU:8 now
where the time goes in v3:
time: 66.6 us; the launch traced here: 66.4 us
  Pallas kernels  65.8 us (99%)
    pallas_call x1, Pallas kernels, body(): pl.pallas_call(kernel, out_shape=shapes, in_specs=[hbm] * 7, out_specs=(v...  64.3 us
    pallas_call x1, Pallas kernels, body(): pl.pallas_call(hand_over, out_shape=shapes, in_specs=[vmem] * 3, out_spec...  1.49 us

profile of v3, /device:TPU:8, one launch (start us, length us, event | category | flops | bytes accessed | tf_op | source)
XLA Modules:
  0.0 66.4 jit_solution(16422291358044318562)
XLA Ops:
  0.6 64.3 %shard_map.94 = (bf16[128,128]{1,0:T(8,128)(2,1)}, bf16[256,128]{1,0:T(8,128)(2,1)}, bf16[64,256]{1,0:T(8,128)(2,1)}) custom-call(bf16[128,2048]{1,0:T(8,128)(2,1)} %hid_hbm.1, bf16[8192,128]{1,0:T(8,128)(2,1)} %bitcast.5, bf16[8,2,128,256]{3,2,1,0:T(8,128)(2,1)} %bitcast.6, bf16[4,128]{1,0:T(4,128)(2,1)} %mw_hbm.1, f32[4,128]{1,0:T(4,128)} %ln_hbm.1, ...), custom_call_target="tpu_custom_call" | custom-call | tf_op jit(solution)/shard_map/pallas_call | solution.py:473
  64.9 1.5 %shard_map.95 = (bf16[128,128]{1,0:T(8,128)(2,1)}, bf16[256,128]{1,0:T(8,128)(2,1)}, bf16[64,256]{1,0:T(8,128)(2,1)}) custom-call(bf16[128,128]{1,0:T(8,128)(2,1)} %get-tuple-element.9.refs_0_, bf16[256,128]{1,0:T(8,128)(2,1)} %get-tuple-element.10.refs_1_, bf16[64,256]{1,0:T(8,128)(2,1)} %get-tuple-element.11.refs_2_), custom_call_target="tpu_custom_call" | custom-call | tf_op jit(solution)/shard_map/pallas_call | solution.py:491

commit v4 on v3

--- a/solution.py
+++ b/solution.py
@@ -12,6 +12,7 @@
 BF, F32 = jnp.bfloat16, jnp.float32
 ZH, Y, ZL, X, C = 4, 8, 2, 4, 2
 D, K, T, V, E = 2048, 4, 128, 256, 128
+SCALE = 2.0**-16
 BULK = 2 * 1024 * 1024
 N_SEND, N_RECV = 4, 102
 
@@ -63,10 +64,10 @@
 
 def kernel(
     hid_hbm, cp_hbm, w_hbm, mw_hbm, ln_hbm, tg_hbm, loss_hbm,
-    hg_ref, pg_ref, vg_ref,
-    hid, cpraw, stage, cp, w, wt, wp, mw_ref, ln_ref, tg_ref, loss_ref, ctx, eb, lgt, lgp, arx,
+    hg_hbm, pg_hbm, vg_hbm,
+    hid, cpraw, stage, cp, w, wt, wp, mw_ref, ln_ref, tg_ref, loss_ref, ctx, eb, lgt, lgu, lgp, arx,
     cgb, zf, sf, r2, sp, zs, rx, ro, pgz, pgs, hx, ht, pp, pc, pn, prx, pst,
-    hpb, hq, hs, hrx, hsum, hz, hzr, vgb, vsb, vrb, vzs, vzr,
+    hpb, hq, hs, hrx, hsum, hz, hzr, vgb, vsb, vrb, vzs, vzr, hgo, pgo, vgo,
     send_sems, recv_sems, local_sems,
 ):
     zh, y = lax.axis_index("zh"), lax.axis_index("y")
@@ -197,12 +198,31 @@
     ids = lax.broadcasted_iota(jnp.int32, (V, T), 0) + voc * V
     hit = ids == tg_ref[...]
     targets = [jnp.sum(jnp.where(hit, eb[:, lanes(k)], 0.0), axis=0, keepdims=True) for k in range(K)]
+    onehot = hit.astype(F32)
+    for k in range(K):
+        grad = jnp.exp(eb[:, lanes(k)] - ln_ref[k : k + 1, :]) - onehot
+        eb[:, lanes(k)] = grad
+        lgu[:, lanes(k)] = (grad * SCALE).astype(BF)
+        if k % 2:
+            net.send(lgu.at[:, lanes(k - 1, 2)], lgp.at[:, lanes(k - 1, 2)], ("lg", k - 1), other)
     arx[0] = jnp.concatenate([*targets, mix_part[:4]], axis=0)
     for i, p in enumerate(voc_peers):
         net.send(arx.at[0], arx.at[i + 1], ("ar",), peer(*p))
-    onehot = hit.astype(F32)
-    for k in range(K):
-        eb[:, lanes(k)] = jnp.exp(eb[:, lanes(k)] - ln_ref[k : k + 1, :]) - onehot
+
+    net.got(wp, ("wp",))
+    w_own = w[:, pl.ds(c, 1)].reshape(8 * E, V)
+    w_partner = wp[...].reshape(8 * E, V)
+    for k in (0, 2):
+        part = mm(w_own, lgu[:, lanes(k, 2)])
+        net.got(lgp.at[:, lanes(k, 2)], ("lg", k))
+        part = part + mm(w_partner, lgp[:, lanes(k, 2)])
+        for j in (k, k + 1):
+            cgb[j] = part[:, (j - k) * T : (j - k + 1) * T].astype(BF).reshape(ZL, X, E, T)
+        for j in (k, k + 1):
+            net.send(cgb.at[j, 1 - zl, xat(2)], zf.at[j], ("zf", j), over)
+            net.send(cgb.at[j, 1 - zl, xat(1)], ro.at[j, 0], ("ro", j), right)
+            net.send(cgb.at[j, 1 - zl, xat(-1)], ro.at[j, 1], ("ro", j), left)
+
     net.got(arx.at[1:16], ("ar",))
     sums = jnp.sum(arx[...], axis=0)
     exp_mix = jnp.exp(sums[4:])
@@ -214,8 +234,7 @@
 
     for k in range(K):
         lgt[:, lanes(k)] = (factor[k : k + 1] * eb[:, lanes(k)]).astype(BF)
-        if k % 2:
-            net.send(lgt.at[:, lanes(k - 1, 2)], lgp.at[:, lanes(k - 1, 2)], ("lg", k - 1), other)
+    factor = factor * (1.0 / SCALE)
 
     for a in range(ZH):
         part = mm_nt(ctx[a * 512 : (a + 1) * 512, :], lgt[...])
@@ -240,18 +259,6 @@
                     chain_send(way, half, dist)
 
     chain_round(0)
-
-    net.got(wp, ("wp",))
-    w_own = w[:, pl.ds(c, 1)].reshape(8 * E, V)
-    for k in (0, 2):
-        net.got(lgp.at[:, lanes(k, 2)], ("lg", k))
-        part = mm(w_own, lgt[:, lanes(k, 2)]) + mm(wp[...].reshape(8 * E, V), lgp[:, lanes(k, 2)])
-        for j in (k, k + 1):
-            cgb[j] = part[:, (j - k) * T : (j - k + 1) * T].astype(BF).reshape(ZL, X, E, T)
-        for j in (k, k + 1):
-            net.send(cgb.at[j, 1 - zl, xat(2)], zf.at[j], ("zf", j), over)
-            net.send(cgb.at[j, 1 - zl, xat(1)], ro.at[j, 0], ("ro", j), right)
-            net.send(cgb.at[j, 1 - zl, xat(-1)], ro.at[j, 1], ("ro", j), left)
 
     def both(a, b):
         return (a[...].astype(F32) + b[...].astype(F32)).astype(BF)
@@ -302,7 +309,7 @@
         net.got(rx.at[k], ("rx", k))
         own = ctx[pl.ds(pl.multiple_of(voc * E, E), E), lanes(k)].astype(F32)
         grad = cgb[k, zl, x].astype(F32) + rx[k, 0].astype(F32) + rx[k, 1].astype(F32) + rx[k, 2].astype(F32)
-        grad = (grad * (1.0 - own * own)).astype(BF)
+        grad = (grad * factor[k : k + 1] * (1.0 - own * own)).astype(BF)
         pgz[k, :, 0:T] = grad
         pgs[k * E : (k + 1) * E, :] = grad
         net.send(pgz.at[k, :, lanes(0)], pgz.at[k, :, lanes(1)], ("pz", 1, k), {"zh": zat(1)})
@@ -369,6 +376,12 @@
     proj(0)
     proj(2)
 
+    outs = []
+
+    def put_out(src, dst):
+        outs.append(pltpu.make_async_copy(src, dst, local_sems.at[10 + len(outs)]))
+        outs[-1].start()
+
     for half in range(2):
         span = slice(2 * half, 2 * half + 2)
         total = vgb[span, y].astype(F32)
@@ -393,19 +406,24 @@
         for i in range(4):
             total = total + prx[k, i].astype(F32)
         pst[pl.ds(k, 64, stride=K), :] = total
-    pg_ref[...] = pst[...].astype(BF)
+    pgo[...] = pst[...].astype(BF)
+    put_out(pgo, pg_hbm)
 
     net.got(hzr, ("hz",))
     total = hsum[zl] + hzr[...].astype(F32)
     mix_grad = jnp.concatenate([mix_grad, jnp.zeros((4, T), F32)], axis=0)
     mix_term = lax.dot_general(mix_grad, mw, TN, precision=lax.Precision.HIGHEST, preferred_element_type=F32)
-    hg_ref[...] = (total.T + mix_term).astype(BF)
+    hgo[...] = (total.T + mix_term).astype(BF)
+    put_out(hgo, hg_hbm)
 
     total = vzs[zh].astype(F32)
     net.got(vzr.at[1:4], ("vz",))
     for dz in range(1, ZH):
         total = total + vzr[dz].astype(F32)
-    vg_ref[...] = total.astype(BF)
+    vgo[...] = total.astype(BF)
+    put_out(vgo, vg_hbm)
+    for copy in outs:
+        copy.wait()
     net.finish()
     assert len(net.bulk) <= N_SEND and len(net.roles) <= N_RECV
 
@@ -416,8 +434,7 @@
 
 
 def body(hidden, mix_weight, comp_proj, vocab_weight, log_normalizer, targets, loss_grad):
-    vmem = pl.BlockSpec(memory_space=pltpu.VMEM)
-    hbm = pl.BlockSpec(memory_space=pl.ANY)
+    hbm, vmem = (pl.BlockSpec(memory_space=m) for m in (pl.ANY, pltpu.VMEM))
     scratch = [
         pltpu.VMEM(shape, dtype)
         for shape, dtype in (
@@ -434,6 +451,7 @@
             ((1, T), F32),
             ((D, K * T), BF),
             ((V, K * T), F32),
+            ((V, K * T), BF),
             ((V, K * T), BF),
             ((V, K * T), BF),
             ((16, 8, T), F32),
@@ -462,9 +480,12 @@
             ((2, 2, 4, 2, 64, V), BF),
             ((ZH, 64, V), BF),
             ((ZH, 64, V), BF),
+            ((T, E), BF),
+            ((64 * K, E), BF),
+            ((64, V), BF),
         )
     ]
-    scratch += [pltpu.SemaphoreType.DMA((N_SEND,)), pltpu.SemaphoreType.DMA((N_RECV,)), pltpu.SemaphoreType.DMA((10,))]
+    scratch += [pltpu.SemaphoreType.DMA((N_SEND,)), pltpu.SemaphoreType.DMA((N_RECV,)), pltpu.SemaphoreType.DMA((13,))]
     shapes = (
         jax.ShapeDtypeStruct((T, E), BF),
         jax.ShapeDtypeStruct((64 * K, E), BF),
@@ -474,7 +495,7 @@
         kernel,
         out_shape=shapes,
         in_specs=[hbm] * 7,
-        out_specs=(vmem, vmem, vmem),
+        out_specs=(hbm,) * 3,
         scratch_shapes=scratch,
         compiler_params=pltpu.CompilerParams(
             collective_id=0, has_side_effects=True, vmem_limit_bytes=56 * 1024 * 1024

time: 66.6 us -> 62.8 us (0.943)
  the two profiles are of different devices: /device:TPU:8 before, /device:TPU:1 now
where the time goes in v4:
time: 62.8 us; the launch traced here: 62.6 us
  Pallas kernels  61.9 us (99%)
  between operations  0.64 us (1%)
    pallas_call x1, Pallas kernels, body(): pl.pallas_call(kernel, out_shape=shapes, in_specs=[hbm] * 7, out_specs=(h...  60.5 us
    pallas_call x1, Pallas kernels, body(): pl.pallas_call(hand_over, out_shape=shapes, in_specs=[vmem] * 3, out_spec...  1.49 us

profile of v4, /device:TPU:1, one launch (start us, length us, event | category | flops | bytes accessed | tf_op | source)
XLA Modules:
  0.0 62.6 jit_solution(7212692869405365808)
XLA Ops:
  0.6 60.5 %shard_map.94 = (bf16[128,128]{1,0:T(8,128)(2,1)}, bf16[256,128]{1,0:T(8,128)(2,1)}, bf16[64,256]{1,0:T(8,128)(2,1)}) custom-call(bf16[128,2048]{1,0:T(8,128)(2,1)} %hid_hbm.1, bf16[8192,128]{1,0:T(8,128)(2,1)} %bitcast.5, bf16[8,2,128,256]{3,2,1,0:T(8,128)(2,1)} %bitcast.6, bf16[4,128]{1,0:T(4,128)(2,1)} %mw_hbm.1, f32[4,128]{1,0:T(4,128)} %ln_hbm.1, ...), custom_call_target="tpu_custom_call" | custom-call | tf_op jit(solution)/shard_map/pallas_call | solution.py:494
  61.1 1.5 %shard_map.95 = (bf16[128,128]{1,0:T(8,128)(2,1)}, bf16[256,128]{1,0:T(8,128)(2,1)}, bf16[64,256]{1,0:T(8,128)(2,1)}) custom-call(bf16[128,128]{1,0:T(8,128)(2,1)} %get-tuple-element.9.refs_0_, bf16[256,128]{1,0:T(8,128)(2,1)} %get-tuple-element.10.refs_1_, bf16[64,256]{1,0:T(8,128)(2,1)} %get-tuple-element.11.refs_2_), custom_call_target="tpu_custom_call" | custom-call | tf_op jit(solution)/shard_map/pallas_call | solution.py:512

commit v5 on v4

--- a/solution.py
+++ b/solution.py
@@ -64,10 +64,10 @@
 
 def kernel(
     hid_hbm, cp_hbm, w_hbm, mw_hbm, ln_hbm, tg_hbm, loss_hbm,
-    hg_hbm, pg_hbm, vg_hbm,
+    hg_ref, pg_ref, vg_ref,
     hid, cpraw, stage, cp, w, wt, wp, mw_ref, ln_ref, tg_ref, loss_ref, ctx, eb, lgt, lgu, lgp, arx,
     cgb, zf, sf, r2, sp, zs, rx, ro, pgz, pgs, hx, ht, pp, pc, pn, prx, pst,
-    hpb, hq, hs, hrx, hsum, hz, hzr, vgb, vsb, vrb, vzs, vzr, hgo, pgo, vgo,
+    hpb, hq, hs, hrx, hsum, hz, hzr, vgb, vsb, vrb, vzs, vzr,
     send_sems, recv_sems, local_sems,
 ):
     zh, y = lax.axis_index("zh"), lax.axis_index("y")
@@ -107,12 +107,11 @@
     small = [(mw_hbm, mw_ref), (ln_hbm, ln_ref), (tg_hbm, tg_ref), (loss_hbm, loss_ref), (w_hbm, w)]
     for i, (src, dst) in enumerate(small):
         loads.append(pltpu.make_async_copy(src, dst, local_sems.at[1 + parts + i]))
-    for load in loads:
-        load.start()
+    for i in (1, 0, *range(2, len(loads))):
+        loads[i].start()
     for device in greeted:
         pl.semaphore_signal(barrier, inc=1, device_id=device, device_id_type=MESH)
 
-    loads[0].wait()
     pre = jnp.zeros((T, K * E), F32)
     for q in range(parts):
         loads[1 + q].wait()
@@ -120,6 +119,8 @@
         span = pl.ds(q * (D // parts), D // parts)
         for k in range(K):
             cp[span, lanes(k)] = stage[pl.ds(k, D // parts, stride=K), :].astype(BF)
+        if q == 0:
+            loads[0].wait()
         pre = pre + mm(hid[:, span], cp[span, :])
     acts = jnp.tanh(pre)
 
@@ -156,11 +157,17 @@
     for j in range(16):
         wt[:, j * 128 : (j + 1) * 128] = w[j // 2, j % 2].T
 
-    def from_side(dl, dx, k):
-        net.got(block(dl, dx, 0, k), ("ag", dl, dx, k))
-        if dl == 0 and (k % 2 == 0) == (dx == -1):
-            push(dl, dx, k, ("ag", 0, 2, k), right if dx == -1 else left)
-        push(dl, dx, k, ("ac", dl, dx), other)
+    def from_side(dx, k):
+        net.got(block(0, dx, 0, k), ("ag", 0, dx, k))
+        if (k % 2 == 0) == (dx == -1):
+            push(0, dx, k, ("ag", 0, 2, k), right if dx == -1 else left)
+        push(0, dx, k, ("ac", 0, dx), other)
+
+    def from_corner(dx):
+        at = (1 - zl) * 8 + xat(dx) * 2 + c
+        whole = ctx.at[pl.ds(pl.multiple_of(at * E, E), E)]
+        net.got(whole, ("ag", 1, dx))
+        net.send(whole, whole, ("ac", 1, dx), other)
 
     def from_far(dl, k):
         net.got(block(dl, 2, 0, k), ("ag", dl, 2, k))
@@ -176,21 +183,21 @@
         eb[...] = part if (dl, dx) == (0, 0) else eb[...] + part
 
     for dx, k in ((-1, 0), (1, 1), (-1, 2), (1, 3)):
-        from_side(0, dx, k)
+        from_side(dx, k)
     for k in range(K):
         net.got(block(1, 0, 0, k), ("ag", 1, 0, k))
-        push(1, 0, k, ("ag", 1, -1, k), right)
-        push(1, 0, k, ("ag", 1, 1, k), left)
+        push(1, 0, k, ("ag", 1, -1), right)
+        push(1, 0, k, ("ag", 1, 1), left)
         push(1, 0, k, ("ac", 1, 0), other)
     for dx, k in ((-1, 1), (1, 0), (-1, 3), (1, 2)):
-        from_side(0, dx, k)
+        from_side(dx, k)
     add_chip(0, 0)
     for k in range(K):
         from_far(0, k)
-    for k, chip in zip(range(K), ((1, 0), (0, -1), (0, 1), (0, 2))):
-        from_side(1, -1, k)
-        from_side(1, 1, k)
+    for chip in ((1, 0), (0, -1), (0, 1), (0, 2)):
         add_chip(*chip)
+    from_corner(-1)
+    from_corner(1)
     for k in range(K):
         from_far(1, k)
     for chip in ((1, -1), (1, 1), (1, 2)):
@@ -223,6 +230,37 @@
             net.send(cgb.at[j, 1 - zl, xat(1)], ro.at[j, 0], ("ro", j), right)
             net.send(cgb.at[j, 1 - zl, xat(-1)], ro.at[j, 1], ("ro", j), left)
 
+    def both(a, b):
+        return (a[...].astype(F32) + b[...].astype(F32)).astype(BF)
+
+    def far(k):
+        net.got(zf.at[k], ("zf", k))
+        sf[k] = both(cgb.at[k, zl, xat(2)], zf.at[k])
+        net.send(sf.at[k], r2.at[k], ("r2", k), left if k % 2 else right)
+
+    def straight(k):
+        if k % 2:
+            net.send(cgb.at[k, zl, xat(1)], rx.at[k, 0], ("rx", k), right)
+        else:
+            net.send(cgb.at[k, zl, xat(-1)], rx.at[k, 1], ("rx", k), left)
+
+    def combine(k):
+        net.got(r2.at[k], ("r2", k))
+        sp[k] = both(cgb.at[k, zl, xat(-1 if k % 2 else 1)], r2.at[k])
+        if k % 2:
+            net.send(sp.at[k], rx.at[k, 1], ("rx", k), left)
+        else:
+            net.send(sp.at[k], rx.at[k, 0], ("rx", k), right)
+
+    def cross(k):
+        net.got(ro.at[k], ("ro", k))
+        zs[k] = (cgb[k, 1 - zl, x].astype(F32) + ro[k, 0].astype(F32) + ro[k, 1].astype(F32)).astype(BF)
+        net.send(zs.at[k], rx.at[k, 2], ("rx", k), over)
+
+    far(0)
+    far(1)
+    straight(0)
+    straight(1)
     net.got(arx.at[1:16], ("ar",))
     sums = jnp.sum(arx[...], axis=0)
     exp_mix = jnp.exp(sums[4:])
@@ -260,37 +298,6 @@
 
     chain_round(0)
 
-    def both(a, b):
-        return (a[...].astype(F32) + b[...].astype(F32)).astype(BF)
-
-    def far(k):
-        net.got(zf.at[k], ("zf", k))
-        sf[k] = both(cgb.at[k, zl, xat(2)], zf.at[k])
-        net.send(sf.at[k], r2.at[k], ("r2", k), left if k % 2 else right)
-
-    def straight(k):
-        if k % 2:
-            net.send(cgb.at[k, zl, xat(1)], rx.at[k, 0], ("rx", k), right)
-        else:
-            net.send(cgb.at[k, zl, xat(-1)], rx.at[k, 1], ("rx", k), left)
-
-    def combine(k):
-        net.got(r2.at[k], ("r2", k))
-        sp[k] = both(cgb.at[k, zl, xat(-1 if k % 2 else 1)], r2.at[k])
-        if k % 2:
-            net.send(sp.at[k], rx.at[k, 1], ("rx", k), left)
-        else:
-            net.send(sp.at[k], rx.at[k, 0], ("rx", k), right)
-
-    def cross(k):
-        net.got(ro.at[k], ("ro", k))
-        zs[k] = (cgb[k, 1 - zl, x].astype(F32) + ro[k, 0].astype(F32) + ro[k, 1].astype(F32)).astype(BF)
-        net.send(zs.at[k], rx.at[k, 2], ("rx", k), over)
-
-    far(0)
-    far(1)
-    straight(0)
-    straight(1)
     far(2)
     far(3)
     straight(2)
@@ -303,8 +310,6 @@
     cross(3)
     combine(2)
     combine(3)
-    chain_round(1)
-
     def pre_grads(k):
         net.got(rx.at[k], ("rx", k))
         own = ctx[pl.ds(pl.multiple_of(voc * E, E), E), lanes(k)].astype(F32)
@@ -315,23 +320,24 @@
         net.send(pgz.at[k, :, lanes(0)], pgz.at[k, :, lanes(1)], ("pz", 1, k), {"zh": zat(1)})
         net.send(pgz.at[k, :, lanes(0)], pgz.at[k, :, lanes(3)], ("pz", 3, k), {"zh": zat(3)})
 
+    net.got(hx.at[1:4, piece(0, 0)], ("hx",))
+
+    def pass_hidden(dx, role, device):
+        net.send(hx.at[1:4, piece(dx, 0)], hx.at[1:4, piece(dx, 0)], role, device)
+
+    for dx in (1, 3, 2):
+        pass_hidden(0, ("hy", 4 - dx), {"x": xat(dx)})
+    pass_hidden(0, ("hc", 0), other)
+    chain_round(1)
     pre_grads(0)
     pre_grads(1)
     pre_grads(2)
     pre_grads(3)
 
-    net.got(hx.at[1:4, piece(0, 0)], ("hx",))
-    row_peers = [(dx, dc) for dx in (1, 3, 2, 0) for dc in range(2) if (dx, dc) != (0, 0)]
-    for dx, dc in row_peers:
-        at = {"x": xat(dx), "c": (c + dc) % 2}
-        net.send(hx.at[1:4, piece(0, 0)], hx.at[1:4, piece(0, 0)], ("hy", (4 - dx) % 4, dc), at)
-
     for j in range(4):
         part = mm(cp[j * 512 : (j + 1) * 512, :], pgs[...])
         hpb[2 * j : 2 * j + 2] = part.astype(BF).reshape(2, 2, 128, T)
     net.send(hpb.at[:, 1 - c], hq, ("hq",), other)
-    chain_round(2)
-
     def z_forward(k):
         net.got(pgz.at[k, :, lanes(1)], ("pz", 1, k))
         if k % 2 == 0:
@@ -345,14 +351,20 @@
         hs[j // X, j % X] = both(hpb.at[j, c], hq.at[j])
     for dx in (1, 3, 2):
         net.send(hs.at[:, xat(dx)], hrx.at[dx - 1], ("hr",), {"x": xat(dx)})
-    for k in range(K):
-        z_forward(k)
-    chain_round(3)
-    for dx, dc in row_peers:
-        net.got(hx.at[1:4, piece(dx, dc)], ("hy", dx, dc))
+    for dx in (1, 3, 2):
+        net.got(hx.at[1:4, piece(dx, 0)], ("hy", dx))
+        pass_hidden(dx, ("hc", dx), other)
+    z_forward(0)
+    z_forward(1)
+    chain_round(2)
+    z_forward(2)
+    z_forward(3)
+    for dx in range(X):
+        net.got(hx.at[1:4, piece(dx, 1)], ("hc", dx))
     for dz in range(ZH):
         ht[:, lanes(dz)] = hx[dz].T
 
+    chain_round(3)
     def proj(k):
         for j in (k, k + 1):
             net.got(pgz.at[j, :, lanes(2)], ("pz", 2, j))
@@ -376,12 +388,6 @@
     proj(0)
     proj(2)
 
-    outs = []
-
-    def put_out(src, dst):
-        outs.append(pltpu.make_async_copy(src, dst, local_sems.at[10 + len(outs)]))
-        outs[-1].start()
-
     for half in range(2):
         span = slice(2 * half, 2 * half + 2)
         total = vgb[span, y].astype(F32)
@@ -391,14 +397,14 @@
         vzs[span] = total.astype(BF)
     for dz in (1, 3, 2):
         net.send(vzs.at[zat(dz)], vzr.at[dz], ("vz",), {"zh": zat(dz)})
-    for k in range(K):
-        proj_on(k)
     net.got(hrx, ("hr",))
     hsum[...] = hs[:, x].astype(F32)
     for i in range(3):
         hsum[...] += hrx[i].astype(F32)
     hz[...] = hsum[1 - zl].astype(BF)
     net.send(hz, hzr, ("hz",), over)
+    for k in range(K):
+        proj_on(k)
 
     for k in range(K):
         net.got(prx.at[k], ("py", k))
@@ -406,31 +412,29 @@
         for i in range(4):
             total = total + prx[k, i].astype(F32)
         pst[pl.ds(k, 64, stride=K), :] = total
-    pgo[...] = pst[...].astype(BF)
-    put_out(pgo, pg_hbm)
+    pg_ref[...] = pst[...].astype(BF)
 
     net.got(hzr, ("hz",))
     total = hsum[zl] + hzr[...].astype(F32)
     mix_grad = jnp.concatenate([mix_grad, jnp.zeros((4, T), F32)], axis=0)
     mix_term = lax.dot_general(mix_grad, mw, TN, precision=lax.Precision.HIGHEST, preferred_element_type=F32)
-    hgo[...] = (total.T + mix_term).astype(BF)
-    put_out(hgo, hg_hbm)
+    hg_ref[...] = (total.T + mix_term).astype(BF)
 
     total = vzs[zh].astype(F32)
     net.got(vzr.at[1:4], ("vz",))
     for dz in range(1, ZH):
         total = total + vzr[dz].astype(F32)
-    vgo[...] = total.astype(BF)
-    put_out(vgo, vg_hbm)
-    for copy in outs:
-        copy.wait()
+    vg_ref[...] = total.astype(BF)
     net.finish()
     assert len(net.bulk) <= N_SEND and len(net.roles) <= N_RECV
 
 
 def hand_over(*refs):
-    for src, dst in zip(refs[:3], refs[3:]):
-        dst[...] = src[...]
+    copies = [pltpu.make_async_copy(refs[i], refs[3 + i], refs[6].at[i]) for i in range(3)]
+    for copy in copies:
+        copy.start()
+    for copy in copies:
+        copy.wait()
 
 
 def body(hidden, mix_weight, comp_proj, vocab_weight, log_normalizer, targets, loss_grad):
@@ -480,12 +484,9 @@
             ((2, 2, 4, 2, 64, V), BF),
             ((ZH, 64, V), BF),
             ((ZH, 64, V), BF),
-            ((T, E), BF),
-            ((64 * K, E), BF),
-            ((64, V), BF),
         )
     ]
-    scratch += [pltpu.SemaphoreType.DMA((N_SEND,)), pltpu.SemaphoreType.DMA((N_RECV,)), pltpu.SemaphoreType.DMA((13,))]
+    scratch += [pltpu.SemaphoreType.DMA((N_SEND,)), pltpu.SemaphoreType.DMA((N_RECV,)), pltpu.SemaphoreType.DMA((10,))]
     shapes = (
         jax.ShapeDtypeStruct((T, E), BF),
         jax.ShapeDtypeStruct((64 * K, E), BF),
@@ -493,9 +494,9 @@
     )
     results = pl.pallas_call(
         kernel,
-        out_shape=shapes,
+        out_shape=tuple(pltpu.VMEM(s.shape, s.dtype) for s in shapes),
         in_specs=[hbm] * 7,
-        out_specs=(hbm,) * 3,
+        out_specs=(vmem,) * 3,
         scratch_shapes=scratch,
         compiler_params=pltpu.CompilerParams(
             collective_id=0, has_side_effects=True, vmem_limit_bytes=56 * 1024 * 1024
@@ -510,8 +511,12 @@
         loss_grad.reshape(1, T),
     )
     hidden_grad, proj_grad, vocab_grad = pl.pallas_call(
-        hand_over, out_shape=shapes, in_specs=[vmem] * 3, out_specs=(vmem,) * 3
-    )(*results)
+        hand_over,
+        out_shape=shapes,
+        in_specs=[vmem] * 3,
+        out_specs=(hbm,) * 3,
+        scratch_shapes=[pltpu.SemaphoreType.DMA((3,))],
+    )(*[pltpu.with_memory_space_constraint(r, pltpu.VMEM) for r in results])
     return hidden_grad, proj_grad.reshape(64, K, E), vocab_grad
 
 

time: 62.8 us -> 61.4 us (0.978)
  Pallas kernels: 61.9 us -> 60.2 us
    pallas_call x1, Pallas kernels: 60.5 us -> 59.6 us  [body(): pl.pallas_call(kernel, out_shape=tuple((pltpu.VMEM(s.shape, s.dtype) for...]
    pallas_call x1, Pallas kernels: 1.49 us -> 0.68 us  [body(): pl.pallas_call(hand_over, out_shape=shapes, in_specs=[vmem] * 3, out_spec...]
where the time goes in v5:
time: 61.4 us; the launch traced here: 60.9 us
  Pallas kernels  60.2 us (98%)
  between operations  0.64 us (1%)
    pallas_call x1, Pallas kernels, body(): pl.pallas_call(kernel, out_shape=tuple((pltpu.VMEM(s.shape, s.dtype) for...  59.6 us

profile of v5, /device:TPU:1, one launch (start us, length us, event | category | flops | bytes accessed | tf_op | source)
XLA Modules:
  0.0 60.9 jit_solution(8877340495563376325)
XLA Ops:
  0.6 59.6 %shard_map.94 = (bf16[128,128]{1,0:T(8,128)(2,1)S(1)}, bf16[256,128]{1,0:T(8,128)(2,1)S(1)}, bf16[64,256]{1,0:T(8,128)(2,1)S(1)}) custom-call(bf16[128,2048]{1,0:T(8,128)(2,1)} %hid_hbm.1, bf16[8192,128]{1,0:T(8,128)(2,1)} %bitcast.5, bf16[8,2,128,256]{3,2,1,0:T(8,128)(2,1)} %bitcast.6, bf16[4,128]{1,0:T(4,128)(2,1)} %mw_hbm.1, f32[4,128]{1,0:T(4,128)} %ln_hbm.1, ...), custom_call_target="tpu_custom_call" | custom-call | tf_op jit(solution)/shard_map/pallas_call | solution.py:495
  60.2 0.7 %shard_map.95 = (bf16[128,128]{1,0:T(8,128)(2,1)}, bf16[256,128]{1,0:T(8,128)(2,1)}, bf16[64,256]{1,0:T(8,128)(2,1)}) custom-call(bf16[128,128]{1,0:T(8,128)(2,1)S(1)} %get-tuple-element.9.refs_0_, bf16[256,128]{1,0:T(8,128)(2,1)S(1)} %get-tuple-element.10.refs_1_, bf16[64,256]{1,0:T(8,128)(2,1)S(1)} %get-tuple-element.11.refs_2_), custom_call_target="tpu_custom_call" | custom-call | tf_op jit(solution)/shard_map/pallas_call | solution.py:513

commit v6 on v0

v6 whole, which is shorter than its diff:
```python
import math

import jax
import jax.numpy as jnp
from jax import lax
from jax.experimental import pallas as pl
from jax.experimental.pallas import tpu as pltpu
from jax.sharding import Mesh
from jax.sharding import PartitionSpec as P

MESH = pl.DeviceIdType.MESH
BF, F32 = jnp.bfloat16, jnp.float32
ZH, Y, ZL, X, C = 4, 8, 2, 4, 2
D, K, T, V, E = 2048, 4, 128, 256, 128
SCALE = 2.0**-16
BULK = 2 * 1024 * 1024
N_SEND, N_RECV = 5, 129

NT = (((1,), (1,)), ((), ()))
TN = (((0,), (0,)), ((), ()))


def mm(a, b):
    return jnp.dot(a, b, preferred_element_type=F32)


def mm_nt(a, b):
    return lax.dot_general(a, b, NT, preferred_element_type=F32)


class Net:
    def __init__(self, send_sems, recv_sems, yard):
        self.send_sems, self.recv_sems, self.yard = send_sems, recv_sems, yard
        self.roles, self.bulk = {}, []

    def slot(self, role):
        return self.recv_sems.at[self.roles.setdefault(role, len(self.roles))]

    def copy(self, src, dst, role, device):
        return pltpu.make_async_remote_copy(
            src_ref=src,
            dst_ref=dst,
            send_sem=self.send_sems.at[max(len(self.bulk), 1) - 1],
            recv_sem=self.slot(role),
            device_id=device,
            device_id_type=MESH,
        )

    def send(self, src, dst, role, device):
        size = math.prod(src.shape) * src.dtype.itemsize
        if not self.bulk or self.bulk[-1] + size > BULK:
            self.bulk.append(0)
        self.bulk[-1] += size
        self.copy(src, dst, role, device).start()

    def got(self, dst, role):
        self.copy(dst, dst, role, {"c": 1 - lax.axis_index("c")}).wait_recv()

    def finish(self):
        for i, size in enumerate(self.bulk):
            sent = self.yard.at[pl.ds(0, size // (E * 2))]
            pltpu.make_async_copy(sent, sent, self.send_sems.at[i]).wait()


def kernel(
    hid_hbm, cp_hbm, w_hbm, mw_hbm, ln_hbm, tg_hbm, loss_hbm,
    hg_ref, pg_ref, vg_ref,
    hid, cpraw, stage, cp, w, wt, mw_ref, ln_ref, tg_ref, loss_ref, mixb, mixs, ctx, eb, lgt, lgu, arx, sumb, sumr,
    cgb, zf, sf, r2, sp, zs, rx, ro, pgz, pgs, hx, ht, pp, pc, pn, prx, pst, pgo, pgr,
    hpb, hq, hs, hrx, hsum, hz, hzr, vgb, vsb, vrb, vzs, vzr, vgo, vgr,
    send_sems, recv_sems, local_sems,
):
    zh, y = lax.axis_index("zh"), lax.axis_index("y")
    zl, x, c = lax.axis_index("zl"), lax.axis_index("x"), lax.axis_index("c")
    chip = zl * X + x
    voc = chip * 2 + c
    net = Net(send_sems, recv_sems, cpraw)

    def xat(dx):
        return lax.rem(x + dx + X, X)

    def yat(dy):
        return lax.rem(y + dy + Y, Y)

    def zat(dz):
        return lax.rem(zh + dz, ZH)

    def lanes(k, n=1):
        return pl.ds(k * T, n * T)

    right, left = {"x": xat(1)}, {"x": xat(-1)}
    up, down = {"y": yat(1)}, {"y": yat(-1)}
    other, over = {"c": 1 - c}, {"zl": 1 - zl}
    chips = [(dl, dx) for dl in range(2) for dx in range(4)][1:]

    barrier = pltpu.get_barrier_semaphore()
    greeted = [{"zl": (zl + dl) % 2, "x": xat(dx)} for dl, dx in chips] + [other]
    greeted += [{"y": yat(dy)} for dy in (1, 2, 3, 5, 6, 7)] + [{"zh": zat(dz)} for dz in range(1, ZH)]
    parts = 4
    rows = D * K // parts
    loads = [pltpu.make_async_copy(hid_hbm, hid, local_sems.at[0])]
    for q in range(parts):
        span = pl.ds(q * rows, rows)
        loads.append(pltpu.make_async_copy(cp_hbm.at[span], cpraw.at[span], local_sems.at[1 + q]))
    small = [(mw_hbm, mw_ref), (ln_hbm, ln_ref), (tg_hbm, tg_ref), (loss_hbm, loss_ref)]
    small += [(w_hbm, w.at[:, pl.ds(pl.multiple_of(c * V, V), V)])]
    for i, (src, dst) in enumerate(small):
        loads.append(pltpu.make_async_copy(src, dst, local_sems.at[1 + parts + i]))
    for i in (1, 0, *range(2, len(loads))):
        loads[i].start()
    for device in greeted:
        pl.semaphore_signal(barrier, inc=1, device_id=device, device_id_type=MESH)

    pre = jnp.zeros((T, K * E), F32)
    for q in range(parts):
        loads[1 + q].wait()
        stage[...] = cpraw[pl.ds(q * rows, rows), :].astype(F32)
        span = pl.ds(q * (D // parts), D // parts)
        for k in range(K):
            cp[span, lanes(k)] = stage[pl.ds(k, D // parts, stride=K), :].astype(BF)
        if q == 0:
            loads[0].wait()
        pre = pre + mm(hid[:, span], cp[span, :])
    acts = jnp.tanh(pre)
    for k in range(K):
        ctx[pl.ds(pl.multiple_of(voc * E, E), E), lanes(k)] = acts[:, k * E : (k + 1) * E].T.astype(BF)

    pl.semaphore_wait(barrier, len(greeted))

    def chip_at(dl, dx):
        return (zl + dl) % 2 * X + xat(dx)

    def block(dl, dx, half, k):
        at = chip_at(dl, dx) * 256 + half * E
        return ctx.at[pl.ds(pl.multiple_of(at, E), E), lanes(k)]

    def half_of(dl, dx, half):
        return ctx.at[pl.ds(pl.multiple_of(chip_at(dl, dx) * 256 + half * E, E), E)]

    def whole(dl, dx):
        return ctx.at[pl.ds(pl.multiple_of(chip_at(dl, dx) * 256, 256), 256)]

    def push(dl, dx, half, k, role, device):
        net.send(block(dl, dx, half, k), block(dl, dx, half, k), role, device)

    def small_loads():
        for i in range(len(small)):
            loads[1 + parts + i].wait()

    def mixing():
        mw = jnp.concatenate([mw_ref[...].astype(F32), jnp.zeros((4, E), F32)], axis=0)
        return mw, mm_nt(mw.astype(BF), hid[:, pl.ds(pl.multiple_of(voc * E, E), E)])

    def turn(start):
        for j in range(16):
            wt[start : start + V, j * 128 : (j + 1) * 128] = w[j * 128 : (j + 1) * 128, start : start + V].T

    def add_chip(dl, dx, n):
        span = pl.ds(pl.multiple_of(chip_at(dl, dx) * 256, 256), 256)
        eb[0:n] += mm(wt[0:n, span], ctx[span, :])

    def add_row(n):
        span = pl.ds(pl.multiple_of(zl * 1024, 1024), 1024)
        eb[0:n] = mm(wt[0:n, span], ctx[span, :])

    def hits(n):
        return (lax.broadcasted_iota(jnp.int32, (n, T), 0) + chip * 512) == tg_ref[...]

    def shares(sums):
        exp_mix = jnp.exp(sums[4:])
        weights = exp_mix / jnp.sum(exp_mix, axis=0, keepdims=True)
        joint = weights * jnp.exp(sums[:4] - ln_ref[...])
        posterior = joint / jnp.sum(joint, axis=0, keepdims=True)
        return loss_ref[...] * posterior, loss_ref[...] * (weights - posterior)

    def both(a, b):
        return (a[...].astype(F32) + b[...].astype(F32)).astype(BF)

    def scaled(factor, start):
        for k in range(K):
            lgt[start : start + V, lanes(k)] = (factor[k : k + 1] * eb[start : start + V, lanes(k)]).astype(BF)

    def vocab(ids):
        for a in range(ZH):
            part = mm_nt(ctx[a * 512 : (a + 1) * 512, :], lgt[ids * V : (ids + 1) * V])
            vgb[ids, a] = part.astype(BF).reshape(Y, 64, V)
        chain_part(ids, 0)

    def chain_send(ids, way, half, dist):
        sign = 1 - 2 * way
        owner = yat(sign * dist)
        src = vgb.at[ids, 2 * half : 2 * half + 2, owner]
        if dist < (4 if half == way else 3):
            got = vrb.at[ids, way, half, dist]
            net.got(got, ("vy", ids, way, half, dist + 1))
            vsb[ids, way, half, dist - 1] = both(src, got)
            src = vsb.at[ids, way, half, dist - 1]
        there = vrb.at[ids, way, half, dist - 1]
        net.send(src, there, ("vy", ids, way, half, dist), up if way == 0 else down)

    def chain_part(ids, n):
        for half in range(2):
            for way in range(2):
                dist = (4 if half == way else 3) - n
                if dist > 0:
                    chain_send(ids, way, half, dist)

    def chain_round(n):
        for ids in range(2):
            chain_part(ids, n)

    def chain_end():
        for ids in range(2):
            for half in range(2):
                span = slice(2 * half, 2 * half + 2)
                total = vgb[ids, span, y].astype(F32)
                for way in range(2):
                    net.got(vrb.at[ids, way, half, 0], ("vy", ids, way, half, 1))
                    total = total + vrb[ids, way, half, 0].astype(F32)
                vzs[ids, span] = total.astype(BF)
            for dz in (2, 1, 3):
                net.send(vzs.at[ids, zat(dz)], vzr.at[ids, dz], ("vz", ids), {"zh": zat(dz)})

    def vocab_out():
        for ids in (1, 0):
            total = vzs[ids, zh].astype(F32)
            net.got(vzr.at[ids, 1:4], ("vz", ids))
            for dz in range(1, ZH):
                total = total + vzr[ids, dz].astype(F32)
            if ids:
                vgo[...] = total.astype(BF)
                net.send(vgo, vgr, ("vgr",), other)
            else:
                vg_ref[...] = total.astype(BF)

    def hidden_part():
        for j in range(4):
            part = mm(cp[j * 512 : (j + 1) * 512, :], pgs[...])
            hpb[2 * j : 2 * j + 2] = part.astype(BF).reshape(2, 2, 128, T)
        net.send(hpb.at[:, 1 - c], hq, ("hq",), other)

    def hidden_x():
        net.got(hq, ("hq",))
        for j in range(8):
            hs[j // X, j % X] = both(hpb.at[j, c], hq.at[j])
        for dx in (1, 3, 2):
            net.send(hs.at[:, xat(dx)], hrx.at[dx - 1], ("hr",), {"x": xat(dx)})

    def hidden_z():
        net.got(hrx, ("hr",))
        hsum[...] = hs[:, x].astype(F32)
        for i in range(3):
            hsum[...] += hrx[i].astype(F32)
        hz[...] = hsum[1 - zl].astype(BF)
        net.send(hz, hzr, ("hz",), over)

    def hidden_out(mix_grad, mw):
        net.got(hzr, ("hz",))
        total = hsum[zl] + hzr[...].astype(F32)
        mix_grad = jnp.concatenate([mix_grad, jnp.zeros((4, T), F32)], axis=0)
        mix_term = lax.dot_general(mix_grad, mw, TN, precision=lax.Precision.HIGHEST, preferred_element_type=F32)
        hg_ref[...] = (total.T + mix_term).astype(BF)

    def leader():
        for k, to_right, to_left in zip(range(K), (0, 2, 1, 3), (1, 3, 0, 2)):
            push(0, 0, 1, to_right, ("ag", 0, -1, 1, to_right), right)
            push(0, 0, 1, to_left, ("ag", 0, 1, 1, to_left), left)
            push(0, 0, 1, k, ("ag", 1, 0, 1, k), over)
            push(0, 0, 1, k, ("ac", 0, 0), other)
        def piece(dx):
            return pl.ds(pl.multiple_of(xat(dx) * 32, 32), 32)

        for k, ways in enumerate((((0,), ()), ((), (1,)), ((2,), ()), ((1, 3), (3, 0, 2)))):
            net.got(block(0, 0, 0, k), ("own", k))
            for j in ways[0]:
                push(0, 0, 0, j, ("ag", 0, -1, 0, j), right)
            for j in ways[1]:
                push(0, 0, 0, j, ("ag", 0, 1, 0, j), left)
            push(0, 0, 0, k, ("ag", 1, 0, 0, k), over)
        for dz in (1, 3, 2):
            span = pl.ds(pl.multiple_of(zat(dz) * 512, 512), 512)
            net.send(hid.at[piece(0), span], hx.at[dz, piece(0)], ("hx",), {"zh": zat(dz)})
        hx[0] = hid[:, pl.ds(pl.multiple_of(zh * 512, 512), 512)]
        small_loads()
        mw, mix_part = mixing()
        turn(V)

        def from_side(half, dx, k):
            net.got(block(0, dx, half, k), ("ag", 0, dx, half, k))
            if (k % 2 == 0) == (dx == -1):
                push(0, dx, half, k, ("ag", 0, 2, half, k), right if dx == -1 else left)
            push(0, dx, half, k, ("ac", 0, dx), other)

        for half in (1, 0):
            for dx, k in ((-1, 0), (1, 1), (-1, 2), (1, 3)):
                from_side(half, dx, k)
            for k in range(K):
                net.got(block(1, 0, half, k), ("ag", 1, 0, half, k))
                push(1, 0, half, k, ("ag", 1, -1), right)
                push(1, 0, half, k, ("ag", 1, 1), left)
                push(1, 0, half, k, ("ac", 1, 0), other)
            for dx, k in ((-1, 1), (1, 0), (-1, 3), (1, 2)):
                from_side(half, dx, k)
        net.got(w.at[:, 0:V], ("ws",))
        turn(0)

        def from_far(half):
            for k in range(K):
                net.got(block(0, 2, half, k), ("ag", 0, 2, half, k))
                push(0, 2, half, k, ("ag", 1, 2, half), over)
                push(0, 2, half, k, ("ac", 0, 2), other)

        from_far(1)
        from_far(0)
        add_row(512)
        add_chip(1, 0, 512)
        for dx in (-1, 1):
            net.got(whole(1, dx), ("ag", 1, dx))
            net.send(whole(1, dx), whole(1, dx), ("ac", 1, dx), other)
            add_chip(1, dx, 512)
        for half in (1, 0):
            net.got(half_of(1, 2, half), ("ag", 1, 2, half))
            net.send(half_of(1, 2, half), half_of(1, 2, half), ("ac", 1, 2), other)
        add_chip(1, 2, 512)

        hit = hits(512)
        onehot = hit.astype(F32)
        targets = [jnp.sum(jnp.where(hit, eb[:, lanes(k)], 0.0), axis=0, keepdims=True) for k in range(K)]
        net.got(mixs, ("mix",))
        arx[0] = jnp.concatenate([*targets, mix_part[:4] + mixs[0:4]], axis=0)
        for i, (dl, dx) in enumerate(chips):
            net.send(arx.at[0], arx.at[i + 1], ("ar",), {"zl": (zl + dl) % 2, "x": xat(dx)})
        for k in range(K):
            grad = jnp.exp(eb[:, lanes(k)] - ln_ref[k : k + 1, :]) - onehot
            eb[:, lanes(k)] = grad
            lgu[:, lanes(k)] = (grad * SCALE).astype(BF)

        for row in (1 - zl, zl):
            for k in (0, 2):
                part = mm(w[pl.ds(pl.multiple_of(row * 1024, 1024), 1024), :], lgu[:, lanes(k, 2)])
                for j in (k, k + 1):
                    cgb[j, row] = part[:, (j - k) * T : (j - k + 1) * T].astype(BF).reshape(X, 2 * E, T)
                if row is zl:
                    continue
                for j in (k, k + 1):
                    net.send(cgb.at[j, 1 - zl, xat(2)], zf.at[j], ("zf", j), over)
                    net.send(cgb.at[j, 1 - zl, xat(1)], ro.at[j, 0], ("ro", j), right)
                    net.send(cgb.at[j, 1 - zl, xat(-1)], ro.at[j, 1], ("ro", j), left)

        def far(k):
            net.got(zf.at[k], ("zf", k))
            sf[k] = both(cgb.at[k, zl, xat(2)], zf.at[k])
            net.send(sf.at[k], r2.at[k], ("r2", k), left if k % 2 else right)

        def straight(k):
            if k % 2:
                net.send(cgb.at[k, zl, xat(1)], rx.at[k, 0], ("rx", k), right)
            else:
                net.send(cgb.at[k, zl, xat(-1)], rx.at[k, 1], ("rx", k), left)

        def combine(k):
            net.got(r2.at[k], ("r2", k))
            sp[k] = both(cgb.at[k, zl, xat(-1 if k % 2 else 1)], r2.at[k])
            if k % 2:
                net.send(sp.at[k], rx.at[k, 1], ("rx", k), left)
            else:
                net.send(sp.at[k], rx.at[k, 0], ("rx", k), right)

        def cross(k):
            net.got(ro.at[k], ("ro", k))
            zs[k] = (cgb[k, 1 - zl, x].astype(F32) + ro[k, 0].astype(F32) + ro[k, 1].astype(F32)).astype(BF)
            net.send(zs.at[k], rx.at[k, 2], ("rx", k), over)

        far(0)
        far(1)
        straight(0)
        straight(1)
        net.got(arx.at[1:8], ("ar",))
        sums = jnp.sum(arx[...], axis=0)
        sumb[...] = sums
        net.send(sumb, sumr, ("sum",), other)
        factor, mix_grad = shares(sums)
        scaled(factor, V)
        net.send(lgt.at[V : 2 * V], lgt.at[V : 2 * V], ("lgt",), other)
        far(2)
        far(3)
        straight(2)
        straight(3)
        factor = factor * (1.0 / SCALE)
        cross(0)
        cross(1)
        combine(0)
        combine(1)
        cross(2)
        cross(3)
        combine(2)
        combine(3)

        def z_send(k):
            net.send(pgz.at[k, :, lanes(0)], pgz.at[k, :, lanes(1)], ("pz", 1, k), {"zh": zat(1)})
            net.send(pgz.at[k, :, lanes(0)], pgz.at[k, :, lanes(3)], ("pz", 3, k), {"zh": zat(3)})

        def pre_grads(k):
            net.got(rx.at[k], ("rx", k))
            own = whole(0, 0)[:, k * T : (k + 1) * T].astype(F32)
            grad = cgb[k, zl, x].astype(F32) + rx[k, 0].astype(F32) + rx[k, 1].astype(F32) + rx[k, 2].astype(F32)
            grad = (grad * factor[k : k + 1] * (1.0 - own * own)).astype(BF)
            pgz[k, :, 0:T] = grad
            z_send(k)
            net.send(pgz.at[k, 0:E, lanes(0)], pgs.at[k * E : (k + 1) * E], ("pgs",), other)
            pgs[k * E : (k + 1) * E, :] = grad[E:]

        net.got(hx.at[1:4, piece(0)], ("hx",))
        for dx in (1, 3, 2):
            net.send(hx.at[1:4, piece(0)], hx.at[1:4, piece(0)], ("hy", 4 - dx), {"x": xat(dx)})
        pre_grads(0)
        pre_grads(1)
        pre_grads(2)
        pre_grads(3)
        hidden_part()

        def z_forward(k):
            side = 3 if k % 2 else 1
            net.got(pgz.at[k, :, lanes(side)], ("pz", side, k))
            net.send(pgz.at[k, :, lanes(side)], pgz.at[k, :, lanes(2)], ("pz", 2, k), {"zh": zat(side)})

        z_forward(0)
        z_forward(1)
        hidden_x()
        z_forward(2)
        z_forward(3)
        for dx in (1, 3, 2):
            net.got(hx.at[1:4, piece(dx)], ("hy", dx))
        for dz in range(ZH):
            ht[:, lanes(dz)] = hx[dz].T

        def proj(k):
            for j in (k, k + 1):
                net.got(pgz.at[j, :, lanes(1 if j % 2 else 3)], ("pz", 1 if j % 2 else 3, j))
                net.got(pgz.at[j, :, lanes(2)], ("pz", 2, j))
            part = mm_nt(ht[...], pgz[k : k + 2].reshape(4 * E, ZH * T))
            for j in (k, k + 1):
                pp[j] = part[:, (j - k) * 2 * E : (j - k + 1) * 2 * E].astype(BF).reshape(Y, 64, 2 * E)
            for j in (k, k + 1):
                sign, far_way, near_way = (-1, down, up) if j % 2 else (1, up, down)
                net.send(pp.at[j, yat(4 * sign)], pn.at[j, 0], ("pn", j), far_way)
                net.send(pp.at[j, yat(2 * sign)], pn.at[j, 1], ("pn", j), far_way)
                net.send(pp.at[j, yat(-3 * sign)], pn.at[j, 2], ("pn", j), near_way)
                net.send(pp.at[j, yat(-sign)], prx.at[j, 3], ("py", j), near_way)

        def proj_on(j):
            sign = -1 if j % 2 else 1
            net.got(pn.at[j], ("pn", j))
            for i, dist in enumerate((3 * sign, sign, -2 * sign)):
                pc[j, i] = both(pp.at[j, yat(dist)], pn.at[j, i])
                net.send(pc.at[j, i], prx.at[j, i], ("py", j), {"y": yat(dist)})

        proj(0)
        proj(2)
        for k in range(K):
            proj_on(k)
        hidden_z()
        for k in range(K):
            net.got(prx.at[k], ("py", k))
            total = pp[k, y].astype(F32)
            for i in range(4):
                total = total + prx[k, i].astype(F32)
            pst[0, pl.ds(k, 64, stride=K), :] = total[:, :E]
            pst[1, pl.ds(k, 64, stride=K), :] = total[:, E:]
        pgo[...] = pst[0].astype(BF)
        net.send(pgo, pgr, ("pgr",), other)
        pg_ref[...] = pst[1].astype(BF)
        hidden_out(mix_grad, mw)
        net.got(vgr, ("vgr",))
        vg_ref[...] = vgr[...]
        net.finish()

    def helper():
        for k in range(K):
            push(0, 0, 0, k, ("own", k), other)
        small_loads()
        net.send(w.at[:, 0:V], w.at[:, 0:V], ("ws",), other)
        mw, mix_part = mixing()
        mixb[...] = mix_part
        net.send(mixb, mixs, ("mix",), other)
        turn(0)
        for dl, dx in ((0, 0), (0, -1), (0, 1), (0, 2), (1, 0), (1, -1), (1, 1), (1, 2)):
            net.got(whole(dl, dx) if (dl, dx) != (0, 0) else half_of(0, 0, 1), ("ac", dl, dx))
            if (dl, dx) == (0, 2):
                add_row(V)
            elif dl == 1:
                add_chip(dl, dx, V)
        onehot = hits(V).astype(F32)
        for k in range(K):
            eb[0:V, lanes(k)] = jnp.exp(eb[0:V, lanes(k)] - ln_ref[k : k + 1, :]) - onehot
        net.got(sumr, ("sum",))
        factor, mix_grad = shares(sumr[...])
        scaled(factor, 0)
        vocab(0)
        net.got(lgt.at[V : 2 * V], ("lgt",))
        vocab(1)
        chain_round(1)
        net.got(pgs, ("pgs",))
        hidden_part()
        chain_round(2)
        hidden_x()
        chain_round(3)
        hidden_z()
        chain_end()
        hidden_out(mix_grad, mw)
        vocab_out()
        net.got(pgr, ("pgr",))
        pg_ref[...] = pgr[...]
        net.finish()

    before = list(net.bulk)
    pl.when(c == 1)(leader)
    net.bulk = before
    pl.when(c == 0)(helper)


def hand_over(*refs):
    copies = [pltpu.make_async_copy(refs[i], refs[3 + i], refs[6].at[i]) for i in range(3)]
    for copy in copies:
        copy.start()
    for copy in copies:
        copy.wait()


def body(hidden, mix_weight, comp_proj, vocab_weight, log_normalizer, targets, loss_grad):
    hbm, vmem = (pl.BlockSpec(memory_space=m) for m in (pl.ANY, pltpu.VMEM))
    scratch = [
        pltpu.VMEM(shape, dtype)
        for shape, dtype in (
            ((T, D), BF),
            ((D * K, E), BF),
            ((D, E), F32),
            ((D, K * E), BF),
            ((D, 2 * V), BF),
            ((2 * V, D), BF),
            ((K, E), BF),
            ((K, T), F32),
            ((1, T), jnp.int32),
            ((1, T), F32),
            ((8, T), F32),
            ((8, T), F32),
            ((D, K * T), BF),
            ((2 * V, K * T), F32),
            ((2 * V, K * T), BF),
            ((2 * V, K * T), BF),
            ((8, 8, T), F32),
            ((8, T), F32),
            ((8, T), F32),
            ((K, ZL, X, 2 * E, T), BF),
            *[((K, 2 * E, T), BF)] * 5,
            ((K, 3, 2 * E, T), BF),
            ((K, 2, 2 * E, T), BF),
            ((K, 2 * E, ZH * T), BF),
            ((K * E, T), BF),
            ((ZH, T, 512), BF),
            ((512, ZH * T), BF),
            ((K, Y, 64, 2 * E), BF),
            ((K, 3, 64, 2 * E), BF),
            ((K, 3, 64, 2 * E), BF),
            ((K, 4, 64, 2 * E), BF),
            ((2, 64 * K, E), F32),
            ((64 * K, E), BF),
            ((64 * K, E), BF),
            ((8, 2, 128, T), BF),
            ((8, 128, T), BF),
            ((ZL, X, 128, T), BF),
            ((3, ZL, 128, T), BF),
            ((ZL, 128, T), F32),
            ((128, T), BF),
            ((128, T), BF),
            ((2, ZH, Y, 64, V), BF),
            ((2, 2, 2, 4, 2, 64, V), BF),
            ((2, 2, 2, 4, 2, 64, V), BF),
            ((2, ZH, 64, V), BF),
            ((2, ZH, 64, V), BF),
            ((64, V), BF),
            ((64, V), BF),
        )
    ]
    scratch += [pltpu.SemaphoreType.DMA((N_SEND,)), pltpu.SemaphoreType.DMA((N_RECV,)), pltpu.SemaphoreType.DMA((10,))]
    shapes = (
        jax.ShapeDtypeStruct((T, E), BF),
        jax.ShapeDtypeStruct((64 * K, E), BF),
        jax.ShapeDtypeStruct((64, V), BF),
    )
    results = pl.pallas_call(
        kernel,
        out_shape=tuple(pltpu.VMEM(s.shape, s.dtype) for s in shapes),
        in_specs=[hbm] * 7,
        out_specs=(vmem,) * 3,
        scratch_shapes=scratch,
        compiler_params=pltpu.CompilerParams(
            collective_id=0, has_side_effects=True, vmem_limit_bytes=56 * 1024 * 1024
        ),
    )(
        hidden,
        comp_proj.reshape(D * K, E),
        vocab_weight,
        mix_weight,
        log_normalizer,
        targets.reshape(1, T),
        loss_grad.reshape(1, T),
    )
    hidden_grad, proj_grad, vocab_grad = pl.pallas_call(
        hand_over,
        out_shape=shapes,
        in_specs=[vmem] * 3,
        out_specs=(hbm,) * 3,
        scratch_shapes=[pltpu.SemaphoreType.DMA((3,))],
    )(*[pltpu.with_memory_space_constraint(r, pltpu.VMEM) for r in results])
    return hidden_grad, proj_grad.reshape(64, K, E), vocab_grad


def solution(mesh):
    split = Mesh(mesh.devices.reshape(ZH, Y, ZL, X, C), ("zh", "y", "zl", "x", "c"))
    tok, voc = ("zh", "y"), ("zl", "x", "c")
    in_specs = (P(tok, None), P(None, voc), P(None, None, voc), P(None, voc), P(None, tok), P(tok), P(tok))
    out_specs = (P(tok, voc), P(tok, None, voc), P(tok, voc))
    return jax.shard_map(body, mesh=split, in_specs=in_specs, out_specs=out_specs, check_vma=False)
```

time: 239 us -> 58.5 us (0.24)
  waiting for transfers between devices: 141 us -> 0 us
  Pallas kernels: 0 us -> 57.8 us
  blocking collectives: 39.6 us -> 0 us
  starting transfers between devices: 16.8 us -> 0 us
  matrix products: 13.6 us -> 0 us
  between operations: 14 us -> 0.64 us
  local copies, waits for them, and re-layouts: 6.79 us -> 0 us
  other arithmetic: 5.54 us -> 0 us
    reduce_scatter x2 -> x0, waiting for transfers between devices: 86.9 us -> none  [own_block(): tiles = lax.psum_scatter(tiles, axes[k], scatter_dimension=0, tiled=True)]
    pallas_call x0 -> x2, Pallas kernels: none -> 57.8 us  [the longest x1 57.1 us: body(): pl.pallas_call(kernel, out_shape=tuple((pltpu.VMEM(s.shape, s.dtype) for...]
    all_gather x1 -> x0, waiting for transfers between devices: 44.2 us -> none  [body(): context_full = lax.all_gather(context_own, 'voc', axis=0, tiled=True)]
    all_to_all x2 -> x0, blocking collectives: 39.6 us -> none  [the longest x1 29.5 us: sent_and_summed(): tiles = lax.all_to_all(split_up(x, dim, count), axis, 0, 0, tiled=True)]
    all_to_all x2 -> x0, starting transfers between devices: 16.7 us -> none  [the longest x1 11.5 us: body(): lax.all_to_all(partial_sum.astype(jnp.bfloat16), TOK, split_axis=0, conca...]
    dot_general x8 -> x0, matrix products: 13.6 us -> none  [the longest x1 3.17 us: body(): jnp.einsum('td,dke->ekt', hidden, comp_proj, preferred_element_type=jnp.f...]
    all_to_all x2 -> x0, waiting for transfers between devices: 9.66 us -> none  [the longest x1 5.49 us: sent_and_summed(): tiles = lax.all_to_all(split_up(x, dim, count), axis, 0, 0, tiled=True)]
    unnamed x1 -> x0, other arithmetic: 3.09 us -> none
  transfers between devices with their start and end apart: 5 -> 0, of which waited for: 5 -> 0; matrix products, arithmetic and copies ran while one was open for 6% -> 0% of each run, Pallas kernels for 0% -> 0%
where the time goes in v6:
time: 58.5 us; the launch traced here: 58.4 us
  Pallas kernels  57.8 us (99%)
  between operations  0.64 us (1%)
    pallas_call x1, Pallas kernels, body(): pl.pallas_call(kernel, out_shape=tuple((pltpu.VMEM(s.shape, s.dtype) for...  57.1 us

profile of v6, /device:TPU:1, one launch (start us, length us, event | category | flops | bytes accessed | tf_op | source)
XLA Modules:
  0.0 58.4 jit_solution(6508251502160525187)
XLA Ops:
  0.6 57.1 %shard_map.94 = (bf16[128,128]{1,0:T(8,128)(2,1)S(1)}, bf16[256,128]{1,0:T(8,128)(2,1)S(1)}, bf16[64,256]{1,0:T(8,128)(2,1)S(1)}) custom-call(bf16[128,2048]{1,0:T(8,128)(2,1)} %hid_hbm.1, bf16[8192,128]{1,0:T(8,128)(2,1)} %bitcast.4, bf16[2048,256]{1,0:T(8,128)(2,1)} %w_hbm.1, bf16[4,128]{1,0:T(4,128)(2,1)} %mw_hbm.1, f32[4,128]{1,0:T(4,128)} %ln_hbm.1, ...), custom_call_target="tpu_custom_call" | custom-call | tf_op jit(solution)/shard_map/pallas_call | solution.py:591
  57.7 0.7 %shard_map.95 = (bf16[128,128]{1,0:T(8,128)(2,1)}, bf16[256,128]{1,0:T(8,128)(2,1)}, bf16[64,256]{1,0:T(8,128)(2,1)}) custom-call(bf16[128,128]{1,0:T(8,128)(2,1)S(1)} %get-tuple-element.9.refs_0_, bf16[256,128]{1,0:T(8,128)(2,1)S(1)} %get-tuple-element.10.refs_1_, bf16[64,256]{1,0:T(8,128)(2,1)S(1)} %get-tuple-element.11.refs_2_), custom_call_target="tpu_custom_call" | custom-call | tf_op jit(solution)/shard_map/pallas_call | solution.py:609

commit v7 on v6

--- a/solution.py
+++ b/solution.py
@@ -14,7 +14,7 @@
 D, K, T, V, E = 2048, 4, 128, 256, 128
 SCALE = 2.0**-16
 BULK = 2 * 1024 * 1024
-N_SEND, N_RECV = 5, 129
+N_SEND, N_RECV = 5, 109
 
 NT = (((1,), (1,)), ((), ()))
 TN = (((0,), (0,)), ((), ()))
@@ -66,7 +66,7 @@
     hid_hbm, cp_hbm, w_hbm, mw_hbm, ln_hbm, tg_hbm, loss_hbm,
     hg_ref, pg_ref, vg_ref,
     hid, cpraw, stage, cp, w, wt, mw_ref, ln_ref, tg_ref, loss_ref, mixb, mixs, ctx, eb, lgt, lgu, arx, sumb, sumr,
-    cgb, zf, sf, r2, sp, zs, rx, ro, pgz, pgs, hx, ht, pp, pc, pn, prx, pst, pgo, pgr,
+    cgb, zf, sf, r2, sp, zs, rx, ro, pgz, pgs, hx, ht, pp, pc, pn, prx, pst, ppo,
     hpb, hq, hs, hrx, hsum, hz, hzr, vgb, vsb, vrb, vzs, vzr, vgo, vgr,
     send_sems, recv_sems, local_sems,
 ):
@@ -95,8 +95,10 @@
 
     barrier = pltpu.get_barrier_semaphore()
     greeted = [{"zl": (zl + dl) % 2, "x": xat(dx)} for dl, dx in chips] + [other]
-    greeted += [{"y": yat(dy)} for dy in (1, 2, 3, 5, 6, 7)] + [{"zh": zat(dz)} for dz in range(1, ZH)]
-    parts = 4
+    greeted += [{"y": yat(dy), "c": a} for dy in (1, 2, 3, 5, 6, 7) for a in (c, 1 - c)]
+    greeted += [{"zh": zat(dz)} for dz in range(1, ZH)]
+    greeted += [{"c": 1 - c, **device} for device in (right, left, over)]
+    parts = 8
     rows = D * K // parts
     loads = [pltpu.make_async_copy(hid_hbm, hid, local_sems.at[0])]
     for q in range(parts):
@@ -120,7 +122,9 @@
             cp[span, lanes(k)] = stage[pl.ds(k, D // parts, stride=K), :].astype(BF)
         if q == 0:
             loads[0].wait()
-        pre = pre + mm(hid[:, span], cp[span, :])
+        if q % 4 == 3:
+            span = pl.ds((q - 3) * (D // parts), D // 2)
+            pre = pre + mm(hid[:, span], cp[span, :])
     acts = jnp.tanh(pre)
     for k in range(K):
         ctx[pl.ds(pl.multiple_of(voc * E, E), E), lanes(k)] = acts[:, k * E : (k + 1) * E].T.astype(BF)
@@ -140,8 +144,14 @@
     def whole(dl, dx):
         return ctx.at[pl.ds(pl.multiple_of(chip_at(dl, dx) * 256, 256), 256)]
 
-    def push(dl, dx, half, k, role, device):
-        net.send(block(dl, dx, half, k), block(dl, dx, half, k), role, device)
+    def push_own(k, role, device):
+        net.send(block(0, 0, c, k), block(0, 0, c, k), role, device)
+
+    def push_both(dl, dx, k, role, device):
+        net.send(whole(dl, dx).at[:, lanes(k)], whole(dl, dx).at[:, lanes(k)], role, device)
+
+    def pass_on(dl, dx):
+        net.send(whole(dl, dx), whole(dl, dx), ("ac", dl, dx), other)
 
     def small_loads():
         for i in range(len(small)):
@@ -261,22 +271,27 @@
         mix_term = lax.dot_general(mix_grad, mw, TN, precision=lax.Precision.HIGHEST, preferred_element_type=F32)
         hg_ref[...] = (total.T + mix_term).astype(BF)
 
+    def proj_out(own):
+        for k in range(K):
+            net.got(prx.at[k], ("py", k))
+            total = own(k).astype(F32)
+            for i in range(4):
+                total = total + prx[k, i].astype(F32)
+            pst[pl.ds(k, 64, stride=K), :] = total
+        pg_ref[...] = pst[...].astype(BF)
+
+    def push_first(to_right, to_left, to_over):
+        for k, k_right, k_left in zip(range(K), (0, 2, 1, 3), (1, 3, 0, 2)):
+            push_own(k_right, ("ag", 0, -1, k_right), to_right)
+            push_own(k_left, ("ag", 0, 1, k_left), to_left)
+            push_own(k, ("ag", 1, 0, k), to_over)
+
     def leader():
-        for k, to_right, to_left in zip(range(K), (0, 2, 1, 3), (1, 3, 0, 2)):
-            push(0, 0, 1, to_right, ("ag", 0, -1, 1, to_right), right)
-            push(0, 0, 1, to_left, ("ag", 0, 1, 1, to_left), left)
-            push(0, 0, 1, k, ("ag", 1, 0, 1, k), over)
-            push(0, 0, 1, k, ("ac", 0, 0), other)
+        push_first(right, left, over)
+        net.send(half_of(0, 0, 1), half_of(0, 0, 1), ("ac", 0, 0), other)
         def piece(dx):
             return pl.ds(pl.multiple_of(xat(dx) * 32, 32), 32)
 
-        for k, ways in enumerate((((0,), ()), ((), (1,)), ((2,), ()), ((1, 3), (3, 0, 2)))):
-            net.got(block(0, 0, 0, k), ("own", k))
-            for j in ways[0]:
-                push(0, 0, 0, j, ("ag", 0, -1, 0, j), right)
-            for j in ways[1]:
-                push(0, 0, 0, j, ("ag", 0, 1, 0, j), left)
-            push(0, 0, 0, k, ("ag", 1, 0, 0, k), over)
         for dz in (1, 3, 2):
             span = pl.ds(pl.multiple_of(zat(dz) * 512, 512), 512)
             net.send(hid.at[piece(0), span], hx.at[dz, piece(0)], ("hx",), {"zh": zat(dz)})
@@ -285,67 +300,64 @@
         mw, mix_part = mixing()
         turn(V)
 
-        def from_side(half, dx, k):
-            net.got(block(0, dx, half, k), ("ag", 0, dx, half, k))
-            if (k % 2 == 0) == (dx == -1):
-                push(0, dx, half, k, ("ag", 0, 2, half, k), right if dx == -1 else left)
-            push(0, dx, half, k, ("ac", 0, dx), other)
-
-        for half in (1, 0):
-            for dx, k in ((-1, 0), (1, 1), (-1, 2), (1, 3)):
-                from_side(half, dx, k)
-            for k in range(K):
-                net.got(block(1, 0, half, k), ("ag", 1, 0, half, k))
-                push(1, 0, half, k, ("ag", 1, -1), right)
-                push(1, 0, half, k, ("ag", 1, 1), left)
-                push(1, 0, half, k, ("ac", 1, 0), other)
-            for dx, k in ((-1, 1), (1, 0), (-1, 3), (1, 2)):
-                from_side(half, dx, k)
+        def arrived(dl, dx, k):
+            net.got(whole(dl, dx).at[:, lanes(k)], ("ag", dl, dx, k))
+
+        for dx, k, device in ((-1, 0, right), (1, 1, left), (-1, 2, right), (1, 3, left)):
+            arrived(0, dx, k)
+            push_both(0, dx, k, ("ag", 0, 2, k), device)
+        for k in range(K):
+            arrived(1, 0, k)
+            push_both(1, 0, k, ("ag", 1, -1), right)
+            push_both(1, 0, k, ("ag", 1, 1), left)
+        for dx, k in ((-1, 1), (1, 0), (-1, 3), (1, 2)):
+            arrived(0, dx, k)
+        for dl, dx in ((0, -1), (0, 1), (1, 0)):
+            pass_on(dl, dx)
         net.got(w.at[:, 0:V], ("ws",))
         turn(0)
 
-        def from_far(half):
-            for k in range(K):
-                net.got(block(0, 2, half, k), ("ag", 0, 2, half, k))
-                push(0, 2, half, k, ("ag", 1, 2, half), over)
-                push(0, 2, half, k, ("ac", 0, 2), other)
-
-        from_far(1)
-        from_far(0)
+        for k in range(K):
+            arrived(0, 2, k)
+            push_both(0, 2, k, ("ag", 1, 2), over)
+        pass_on(0, 2)
+        net.got(half_of(0, 0, 0), ("own",))
         add_row(512)
         add_chip(1, 0, 512)
-        for dx in (-1, 1):
+        for dx in (-1, 1, 2):
             net.got(whole(1, dx), ("ag", 1, dx))
-            net.send(whole(1, dx), whole(1, dx), ("ac", 1, dx), other)
+            pass_on(1, dx)
             add_chip(1, dx, 512)
-        for half in (1, 0):
-            net.got(half_of(1, 2, half), ("ag", 1, 2, half))
-            net.send(half_of(1, 2, half), half_of(1, 2, half), ("ac", 1, 2), other)
-        add_chip(1, 2, 512)
 
         hit = hits(512)
         onehot = hit.astype(F32)
+
+        def grads(k):
+            return jnp.exp(eb[:, lanes(k)] - ln_ref[k : k + 1, :]) - onehot
+
         targets = [jnp.sum(jnp.where(hit, eb[:, lanes(k)], 0.0), axis=0, keepdims=True) for k in range(K)]
         net.got(mixs, ("mix",))
         arx[0] = jnp.concatenate([*targets, mix_part[:4] + mixs[0:4]], axis=0)
         for i, (dl, dx) in enumerate(chips):
             net.send(arx.at[0], arx.at[i + 1], ("ar",), {"zl": (zl + dl) % 2, "x": xat(dx)})
-        for k in range(K):
-            grad = jnp.exp(eb[:, lanes(k)] - ln_ref[k : k + 1, :]) - onehot
-            eb[:, lanes(k)] = grad
-            lgu[:, lanes(k)] = (grad * SCALE).astype(BF)
-
-        for row in (1 - zl, zl):
-            for k in (0, 2):
-                part = mm(w[pl.ds(pl.multiple_of(row * 1024, 1024), 1024), :], lgu[:, lanes(k, 2)])
-                for j in (k, k + 1):
-                    cgb[j, row] = part[:, (j - k) * T : (j - k + 1) * T].astype(BF).reshape(X, 2 * E, T)
-                if row is zl:
-                    continue
-                for j in (k, k + 1):
-                    net.send(cgb.at[j, 1 - zl, xat(2)], zf.at[j], ("zf", j), over)
-                    net.send(cgb.at[j, 1 - zl, xat(1)], ro.at[j, 0], ("ro", j), right)
-                    net.send(cgb.at[j, 1 - zl, xat(-1)], ro.at[j, 1], ("ro", j), left)
+
+        def part_of(row, k):
+            part = mm(w[pl.ds(pl.multiple_of(row * 1024, 1024), 1024), :], lgu[:, lanes(k, 2)])
+            for j in (k, k + 1):
+                cgb[j, row] = part[:, (j - k) * T : (j - k + 1) * T].astype(BF).reshape(X, 2 * E, T)
+
+        for k in (0, 2):
+            for j in (k, k + 1):
+                lgu[:, lanes(j)] = (grads(j) * SCALE).astype(BF)
+            part_of(1 - zl, k)
+            for j in (k, k + 1):
+                net.send(cgb.at[j, 1 - zl, xat(2)], zf.at[j], ("zf", j), over)
+                net.send(cgb.at[j, 1 - zl, xat(1)], ro.at[j, 0], ("ro", j), right)
+                net.send(cgb.at[j, 1 - zl, xat(-1)], ro.at[j, 1], ("ro", j), left)
+        part_of(zl, 0)
+        part_of(zl, 2)
+        for k in range(K):
+            eb[:, lanes(k)] = grads(k)
 
         def far(k):
             net.got(zf.at[k], ("zf", k))
@@ -434,6 +446,10 @@
         for dz in range(ZH):
             ht[:, lanes(dz)] = hx[dz].T
 
+        def give(src, j, i, dist):
+            net.send(src.at[:, 0:E], prx.at[j, i], ("py", j), {"y": yat(dist), **other})
+            net.send(src.at[:, E : 2 * E], prx.at[j, i], ("py", j), {"y": yat(dist)})
+
         def proj(k):
             for j in (k, k + 1):
                 net.got(pgz.at[j, :, lanes(1 if j % 2 else 3)], ("pz", 1 if j % 2 else 3, j))
@@ -446,38 +462,30 @@
                 net.send(pp.at[j, yat(4 * sign)], pn.at[j, 0], ("pn", j), far_way)
                 net.send(pp.at[j, yat(2 * sign)], pn.at[j, 1], ("pn", j), far_way)
                 net.send(pp.at[j, yat(-3 * sign)], pn.at[j, 2], ("pn", j), near_way)
-                net.send(pp.at[j, yat(-sign)], prx.at[j, 3], ("py", j), near_way)
+                give(pp.at[j, yat(-sign)], j, 3, -sign)
+                net.send(pp.at[j, y, :, 0:E], ppo.at[j], ("po",), other)
 
         def proj_on(j):
             sign = -1 if j % 2 else 1
             net.got(pn.at[j], ("pn", j))
             for i, dist in enumerate((3 * sign, sign, -2 * sign)):
                 pc[j, i] = both(pp.at[j, yat(dist)], pn.at[j, i])
-                net.send(pc.at[j, i], prx.at[j, i], ("py", j), {"y": yat(dist)})
+                give(pc.at[j, i], j, i, dist)
 
         proj(0)
         proj(2)
         for k in range(K):
             proj_on(k)
         hidden_z()
-        for k in range(K):
-            net.got(prx.at[k], ("py", k))
-            total = pp[k, y].astype(F32)
-            for i in range(4):
-                total = total + prx[k, i].astype(F32)
-            pst[0, pl.ds(k, 64, stride=K), :] = total[:, :E]
-            pst[1, pl.ds(k, 64, stride=K), :] = total[:, E:]
-        pgo[...] = pst[0].astype(BF)
-        net.send(pgo, pgr, ("pgr",), other)
-        pg_ref[...] = pst[1].astype(BF)
         hidden_out(mix_grad, mw)
         net.got(vgr, ("vgr",))
         vg_ref[...] = vgr[...]
+        proj_out(lambda k: pp[k, y, :, E : 2 * E])
         net.finish()
 
     def helper():
-        for k in range(K):
-            push(0, 0, 0, k, ("own", k), other)
+        push_first({**right, **other}, {**left, **other}, {**over, **other})
+        net.send(half_of(0, 0, 0), half_of(0, 0, 0), ("own",), other)
         small_loads()
         net.send(w.at[:, 0:V], w.at[:, 0:V], ("ws",), other)
         mw, mix_part = mixing()
@@ -509,8 +517,8 @@
         chain_end()
         hidden_out(mix_grad, mw)
         vocab_out()
-        net.got(pgr, ("pgr",))
-        pg_ref[...] = pgr[...]
+        net.got(ppo, ("po",))
+        proj_out(lambda k: ppo[k])
         net.finish()
 
     before = list(net.bulk)
@@ -534,7 +542,7 @@
         for shape, dtype in (
             ((T, D), BF),
             ((D * K, E), BF),
-            ((D, E), F32),
+            ((D // 2, E), F32),
             ((D, K * E), BF),
             ((D, 2 * V), BF),
             ((2 * V, D), BF),
@@ -562,10 +570,9 @@
             ((K, Y, 64, 2 * E), BF),
             ((K, 3, 64, 2 * E), BF),
             ((K, 3, 64, 2 * E), BF),
-            ((K, 4, 64, 2 * E), BF),
-            ((2, 64 * K, E), F32),
-            ((64 * K, E), BF),
-            ((64 * K, E), BF),
+            ((K, 4, 64, E), BF),
+            ((64 * K, E), F32),
+            ((K, 64, E), BF),
             ((8, 2, 128, T), BF),
             ((8, 128, T), BF),
             ((ZL, X, 128, T), BF),
@@ -582,7 +589,7 @@
             ((64, V), BF),
         )
     ]
-    scratch += [pltpu.SemaphoreType.DMA((N_SEND,)), pltpu.SemaphoreType.DMA((N_RECV,)), pltpu.SemaphoreType.DMA((10,))]
+    scratch += [pltpu.SemaphoreType.DMA((N_SEND,)), pltpu.SemaphoreType.DMA((N_RECV,)), pltpu.SemaphoreType.DMA((14,))]
     shapes = (
         jax.ShapeDtypeStruct((T, E), BF),
         jax.ShapeDtypeStruct((64 * K, E), BF),

time: 58.5 us -> 58.4 us (level)
  no operation moved by 1% of the time
where the time goes in v7:
time: 58.4 us; the launch traced here: 58.2 us
  Pallas kernels  57.6 us (99%)
  between operations  0.64 us (1%)
    pallas_call x1, Pallas kernels, body(): pl.pallas_call(kernel, out_shape=tuple((pltpu.VMEM(s.shape, s.dtype) for...  56.9 us

profile of v7, /device:TPU:1, one launch (start us, length us, event | category | flops | bytes accessed | tf_op | source)
XLA Modules:
  0.0 58.2 jit_solution(5817448901994561845)
XLA Ops:
  0.6 56.9 %shard_map.94 = (bf16[128,128]{1,0:T(8,128)(2,1)S(1)}, bf16[256,128]{1,0:T(8,128)(2,1)S(1)}, bf16[64,256]{1,0:T(8,128)(2,1)S(1)}) custom-call(bf16[128,2048]{1,0:T(8,128)(2,1)} %hid_hbm.1, bf16[8192,128]{1,0:T(8,128)(2,1)} %bitcast.4, bf16[2048,256]{1,0:T(8,128)(2,1)} %w_hbm.1, bf16[4,128]{1,0:T(4,128)(2,1)} %mw_hbm.1, f32[4,128]{1,0:T(4,128)} %ln_hbm.1, ...), custom_call_target="tpu_custom_call" | custom-call | tf_op jit(solution)/shard_map/pallas_call | solution.py:598
  57.6 0.7 %shard_map.95 = (bf16[128,128]{1,0:T(8,128)(2,1)}, bf16[256,128]{1,0:T(8,128)(2,1)}, bf16[64,256]{1,0:T(8,128)(2,1)}) custom-call(bf16[128,128]{1,0:T(8,128)(2,1)S(1)} %get-tuple-element.9.refs_0_, bf16[256,128]{1,0:T(8,128)(2,1)S(1)} %get-tuple-element.10.refs_1_, bf16[64,256]{1,0:T(8,128)(2,1)S(1)} %get-tuple-element.11.refs_2_), custom_call_target="tpu_custom_call" | custom-call | tf_op jit(solution)/shard_map/pallas_call | solution.py:616

commit v8 on v7

--- a/solution.py
+++ b/solution.py
@@ -450,20 +450,16 @@
             net.send(src.at[:, 0:E], prx.at[j, i], ("py", j), {"y": yat(dist), **other})
             net.send(src.at[:, E : 2 * E], prx.at[j, i], ("py", j), {"y": yat(dist)})
 
-        def proj(k):
-            for j in (k, k + 1):
-                net.got(pgz.at[j, :, lanes(1 if j % 2 else 3)], ("pz", 1 if j % 2 else 3, j))
-                net.got(pgz.at[j, :, lanes(2)], ("pz", 2, j))
-            part = mm_nt(ht[...], pgz[k : k + 2].reshape(4 * E, ZH * T))
-            for j in (k, k + 1):
-                pp[j] = part[:, (j - k) * 2 * E : (j - k + 1) * 2 * E].astype(BF).reshape(Y, 64, 2 * E)
-            for j in (k, k + 1):
-                sign, far_way, near_way = (-1, down, up) if j % 2 else (1, up, down)
-                net.send(pp.at[j, yat(4 * sign)], pn.at[j, 0], ("pn", j), far_way)
-                net.send(pp.at[j, yat(2 * sign)], pn.at[j, 1], ("pn", j), far_way)
-                net.send(pp.at[j, yat(-3 * sign)], pn.at[j, 2], ("pn", j), near_way)
-                give(pp.at[j, yat(-sign)], j, 3, -sign)
-                net.send(pp.at[j, y, :, 0:E], ppo.at[j], ("po",), other)
+        def proj(j):
+            net.got(pgz.at[j, :, lanes(1 if j % 2 else 3)], ("pz", 1 if j % 2 else 3, j))
+            net.got(pgz.at[j, :, lanes(2)], ("pz", 2, j))
+            pp[j] = mm_nt(ht[...], pgz[j]).astype(BF).reshape(Y, 64, 2 * E)
+            sign, far_way, near_way = (-1, down, up) if j % 2 else (1, up, down)
+            net.send(pp.at[j, yat(4 * sign)], pn.at[j, 0], ("pn", j), far_way)
+            net.send(pp.at[j, yat(2 * sign)], pn.at[j, 1], ("pn", j), far_way)
+            net.send(pp.at[j, yat(-3 * sign)], pn.at[j, 2], ("pn", j), near_way)
+            give(pp.at[j, yat(-sign)], j, 3, -sign)
+            net.send(pp.at[j, y, :, 0:E], ppo.at[j], ("po",), other)
 
         def proj_on(j):
             sign = -1 if j % 2 else 1
@@ -473,7 +469,9 @@
                 give(pc.at[j, i], j, i, dist)
 
         proj(0)
+        proj(1)
         proj(2)
+        proj(3)
         for k in range(K):
             proj_on(k)
         hidden_z()

time: 58.4 us -> 57.6 us (0.986)
  Pallas kernels: 57.6 us -> 56.9 us
    pallas_call x1, Pallas kernels: 56.9 us -> 56.2 us  [body(): pl.pallas_call(kernel, out_shape=tuple((pltpu.VMEM(s.shape, s.dtype) for...]
where the time goes in v8:
time: 57.6 us; the launch traced here: 57.5 us
  Pallas kernels  56.9 us (99%)
  between operations  0.64 us (1%)
    pallas_call x1, Pallas kernels, body(): pl.pallas_call(kernel, out_shape=tuple((pltpu.VMEM(s.shape, s.dtype) for...  56.2 us

profile of v8, /device:TPU:1, one launch (start us, length us, event | category | flops | bytes accessed | tf_op | source)
XLA Modules:
  0.0 57.5 jit_solution(18087630553277386673)
XLA Ops:
  0.6 56.2 %shard_map.94 = (bf16[128,128]{1,0:T(8,128)(2,1)S(1)}, bf16[256,128]{1,0:T(8,128)(2,1)S(1)}, bf16[64,256]{1,0:T(8,128)(2,1)S(1)}) custom-call(bf16[128,2048]{1,0:T(8,128)(2,1)} %hid_hbm.1, bf16[8192,128]{1,0:T(8,128)(2,1)} %bitcast.4, bf16[2048,256]{1,0:T(8,128)(2,1)} %w_hbm.1, bf16[4,128]{1,0:T(4,128)(2,1)} %mw_hbm.1, f32[4,128]{1,0:T(4,128)} %ln_hbm.1, ...), custom_call_target="tpu_custom_call" | custom-call | tf_op jit(solution)/shard_map/pallas_call | solution.py:596
  56.8 0.7 %shard_map.95 = (bf16[128,128]{1,0:T(8,128)(2,1)}, bf16[256,128]{1,0:T(8,128)(2,1)}, bf16[64,256]{1,0:T(8,128)(2,1)}) custom-call(bf16[128,128]{1,0:T(8,128)(2,1)S(1)} %get-tuple-element.9.refs_0_, bf16[256,128]{1,0:T(8,128)(2,1)S(1)} %get-tuple-element.10.refs_1_, bf16[64,256]{1,0:T(8,128)(2,1)S(1)} %get-tuple-element.11.refs_2_), custom_call_target="tpu_custom_call" | custom-call | tf_op jit(solution)/shard_map/pallas_call | solution.py:614

commit v9 on v8

--- a/solution.py
+++ b/solution.py
@@ -438,9 +438,9 @@
 
         z_forward(0)
         z_forward(1)
-        hidden_x()
         z_forward(2)
         z_forward(3)
+        hidden_x()
         for dx in (1, 3, 2):
             net.got(hx.at[1:4, piece(dx)], ("hy", dx))
         for dz in range(ZH):

time: 57.6 us -> 57.6 us (level)
  no operation moved by 1% of the time
where the time goes in v9:
time: 57.6 us; the launch traced here: 57.5 us
  Pallas kernels  56.9 us (99%)
  between operations  0.64 us (1%)
    pallas_call x1, Pallas kernels, body(): pl.pallas_call(kernel, out_shape=tuple((pltpu.VMEM(s.shape, s.dtype) for...  56.2 us

profile of v9, /device:TPU:1, one launch (start us, length us, event | category | flops | bytes accessed | tf_op | source)
XLA Modules:
  0.0 57.5 jit_solution(13600455050609060007)
XLA Ops:
  0.6 56.2 %shard_map.94 = (bf16[128,128]{1,0:T(8,128)(2,1)S(1)}, bf16[256,128]{1,0:T(8,128)(2,1)S(1)}, bf16[64,256]{1,0:T(8,128)(2,1)S(1)}) custom-call(bf16[128,2048]{1,0:T(8,128)(2,1)} %hid_hbm.1, bf16[8192,128]{1,0:T(8,128)(2,1)} %bitcast.4, bf16[2048,256]{1,0:T(8,128)(2,1)} %w_hbm.1, bf16[4,128]{1,0:T(4,128)(2,1)} %mw_hbm.1, f32[4,128]{1,0:T(4,128)} %ln_hbm.1, ...), custom_call_target="tpu_custom_call" | custom-call | tf_op jit(solution)/shard_map/pallas_call | solution.py:596
  56.8 0.7 %shard_map.95 = (bf16[128,128]{1,0:T(8,128)(2,1)}, bf16[256,128]{1,0:T(8,128)(2,1)}, bf16[64,256]{1,0:T(8,128)(2,1)}) custom-call(bf16[128,128]{1,0:T(8,128)(2,1)S(1)} %get-tuple-element.9.refs_0_, bf16[256,128]{1,0:T(8,128)(2,1)S(1)} %get-tuple-element.10.refs_1_, bf16[64,256]{1,0:T(8,128)(2,1)S(1)} %get-tuple-element.11.refs_2_), custom_call_target="tpu_custom_call" | custom-call | tf_op jit(solution)/shard_map/pallas_call | solution.py:614
